TPU v7x, 32 devices: a whole 2x2x4 slice. The times are simulated.
32 devices in a mesh: clients: 16 (over z, y, core), fsdp: 2 (over x).
Axes of the slice: x: 2, y: 2, z: 4, core: 2. Of those that a mesh axis runs over, the one named last changes fastest.
Arguments:
- token_ids: int32 [16, 1280], P('clients', 'fsdp'), may hold values from 0 to 16383
- target: bfloat16 [16, 1280, 768], P('clients', 'fsdp'), may hold values from -6 to 6
- embedding: bfloat16 [16384, 768], P(None, 'fsdp'), may hold values from -6 to 6
- norm_gain: float32 [768], replicated, may hold values from 0.1 to 1.9
- global_model: float32 [3, 768, 1024], P(None, 'fsdp', 'clients'), may hold values from -0.21875 to 0.21875
- global_control: float32 [3, 768, 1024], P(None, 'fsdp', 'clients'), may hold values from -140 to 140
- client_control: float32 [16, 3, 768, 1024], P('clients', None, 'fsdp'), may hold values from -150 to 150
- local_steps: int32 [16], replicated, may hold values from 1 to 2
- client_weight: int32 [16], replicated, may hold values from 1 to 4
Outputs:
- server_step: float32 [3, 768, 1024], P(None, 'fsdp', 'clients')
- server_control: float32 [3, 768, 1024], P(None, 'fsdp', 'clients')
- client_update: float32 [16, 3, 768, 1024], P('clients', None, 'fsdp')
All inputs are finite; a program needn't handle non-finite values.
Results may differ from a plain program's by a relative error of at most 0.025.
Values may be sent and summed in bfloat16 or wider, within the bound.
A program may use at most 128 MiB of HBM per device.

v0:
```python
import functools
import math

import jax
import jax.numpy as jnp
from jax import lax
from jax.experimental import pallas as pl
from jax.experimental.pallas import tpu as pltpu
from jax.sharding import PartitionSpec as P

LOCAL = 2


learning_rate = 0.005
norm_eps = 1e-06


def gelu_pair(pre_act):
    return jax.vjp(lambda inputs: jax.nn.gelu(inputs, approximate=True), pre_act)


def contract_rows(left, right):
    return lax.dot_general(
        left, right, (((0,), (0,)), ((), ())), preferred_element_type=jnp.float32
    )


def pack_owners(array, owners):
    parts, rows, columns = array.shape
    width = columns // owners
    split = array.reshape(parts, 2, rows // 2, owners, width)
    return split.transpose(3, 0, 2, 1, 4).reshape(owners, parts, rows // 2, 2 * width)


def unpack_owner(array):
    parts, half, width = array.shape
    split = array.reshape(parts, half, 2, width // 2)
    return split.transpose(0, 2, 1, 3).reshape(parts, 2 * half, width // 2)


def general_body(
    token_ids,
    target,
    embedding,
    norm_gain,
    global_model,
    global_control,
    client_control,
    local_steps,
    client_weight,
):
    n_clients = lax.axis_size("clients")
    n_fsdp = lax.axis_size("fsdp")
    client_index = lax.axis_index("clients")
    fsdp_index = lax.axis_index("fsdp")
    paired = n_fsdp == 2 and n_clients % 2 == 0
    if paired:
        core = client_index % 2
        role_client = client_index - core + fsdp_index
        block = core
        swap_pairs = [
            (c * 2 + f, ((c - c % 2) + f) * 2 + c % 2) for c in range(n_clients) for f in range(2)
        ]
        core_pairs = [(c, c ^ 1) for c in range(n_clients)]
    else:
        role_client = client_index
        block = fsdp_index

    def swap_roles(array):
        if not paired:
            return array
        return lax.ppermute(array, ("clients", "fsdp"), swap_pairs)

    def gather_rows(array):
        if not paired:
            return lax.all_gather(array, "fsdp", axis=0, tiled=True)
        other = lax.ppermute(array, "clients", core_pairs)
        return jnp.concatenate(
            [jnp.where(core == 0, array, other), jnp.where(core == 0, other, array)], axis=0
        )

    def reduce_rows(term):
        if not paired:
            return lax.psum_scatter(term, "fsdp", scatter_dimension=0, tiled=True).astype(
                jnp.float32
            )
        rows = term.shape[0] // 2
        own = lax.dynamic_slice_in_dim(term, core * rows, rows, axis=0)
        sent = lax.dynamic_slice_in_dim(term, (1 - core) * rows, rows, axis=0)
        received = lax.ppermute(sent, "clients", core_pairs)
        return own.astype(jnp.float32) + received.astype(jnp.float32)

    tok_rows = target.shape[1]
    group_rows = tok_rows * n_fsdp
    loss_scale = 1.0 / math.sqrt(group_rows)
    all_ids = lax.all_gather(swap_roles(token_ids), "fsdp", axis=1, tiled=True)
    emb_columns = jnp.take(embedding, all_ids[0], axis=0)
    embedded = lax.all_to_all(emb_columns, "fsdp", split_axis=0, concat_axis=1, tiled=True)
    widened = embedded.astype(jnp.float32)
    inv_norm = lax.rsqrt(jnp.mean(widened * widened, axis=1, keepdims=True) + norm_eps)
    normed = (widened * inv_norm * norm_gain).astype(jnp.bfloat16)
    target_rows = swap_roles(target[0]).astype(jnp.float32)
    model_columns = lax.all_gather(
        global_model.astype(jnp.bfloat16), "fsdp", axis=1, tiled=True
    )
    model_full = lax.all_gather(model_columns, "clients", axis=2, tiled=True)
    control_rows = lax.all_gather(
        global_control.astype(jnp.bfloat16), "clients", axis=2, tiled=True
    ).astype(global_control.dtype)
    slots = jnp.arange(local_steps.shape[0])
    step_count = jnp.sum(jnp.where(slots == client_index, local_steps, 0))
    role_steps = jnp.sum(jnp.where(slots == role_client, local_steps, 0))
    own_weight = jnp.sum(jnp.where(slots == client_index, client_weight, 0)).astype(jnp.float32)
    weight_total = jnp.sum(client_weight).astype(jnp.float32)
    correction = control_rows - client_control[0]
    parts, rows = correction.shape[0], correction.shape[1]
    role_correction = [
        swap_roles(correction[part].astype(jnp.bfloat16)).astype(jnp.float32)
        for part in range(parts)
    ]
    role_model = lax.dynamic_slice_in_dim(model_full, block * rows, rows, axis=1).astype(
        jnp.float32
    )
    gathered = [model_full[part] for part in range(parts)]
    pseudo = [jnp.zeros_like(role_correction[part]) for part in range(parts)]
    summed = [jnp.zeros_like(role_correction[part]) for part in range(parts)]
    for local_step in range(LOCAL):
        if local_step > 0:
            gathered = [
                gather_rows(
                    (role_model[part] - learning_rate * pseudo[part]).astype(jnp.bfloat16)
                )
                for part in range(parts)
            ]
        gate_pre = jnp.dot(normed, gathered[0], preferred_element_type=jnp.float32)
        up_pre = jnp.dot(normed, gathered[1], preferred_element_type=jnp.float32)
        gate_act, gelu_back = gelu_pair(gate_pre)
        hidden = (gate_act * up_pre).astype(jnp.bfloat16)
        projected = lax.dot_general(
            hidden, gathered[2], (((1,), (1,)), ((), ())), preferred_element_type=jnp.float32
        )
        out_grad = ((widened + projected - target_rows) * loss_scale).astype(jnp.bfloat16)
        outer_term = contract_rows(out_grad, hidden).astype(jnp.bfloat16)
        hidden_grad = jnp.dot(out_grad, gathered[2], preferred_element_type=jnp.float32)
        gate_grad = gelu_back(hidden_grad * up_pre)[0].astype(jnp.bfloat16)
        up_grad = (hidden_grad * gate_act).astype(jnp.bfloat16)
        gate_term = contract_rows(normed, gate_grad).astype(jnp.bfloat16)
        up_term = contract_rows(normed, up_grad).astype(jnp.bfloat16)
        grads = [reduce_rows(term) for term in (gate_term, up_term, outer_term)]
        step_mask = (local_step < role_steps).astype(jnp.float32)
        for part in range(parts):
            pseudo[part] = pseudo[part] + step_mask * (grads[part] + role_correction[part])
            summed[part] = summed[part] + step_mask * grads[part]
    own_grads = jnp.stack(
        [swap_roles(summed[part].astype(jnp.bfloat16)).astype(jnp.float32) for part in range(parts)]
    )
    taken = jnp.sum((jnp.arange(LOCAL) < step_count).astype(jnp.float32))
    own_pseudo = own_grads + taken * correction
    update = client_control[0] - control_rows + own_pseudo / step_count.astype(jnp.float32)
    packed = jnp.concatenate(
        [
            pack_owners((own_weight * own_pseudo).astype(jnp.bfloat16), n_clients),
            pack_owners((own_weight * update).astype(jnp.bfloat16), n_clients),
        ],
        axis=1,
    )
    sums = lax.psum_scatter(packed, "clients", scatter_dimension=0, tiled=True)[0]
    sums = unpack_owner(sums).astype(jnp.float32) / weight_total
    return (sums[:parts], sums[parts:], update[None])


MESH = pl.DeviceIdType.MESH
TILE = 256
BF = jnp.bfloat16
F32 = jnp.float32


def gelu_parts(x):
    cubic = 0.044715
    scale = math.sqrt(2.0 / math.pi)
    square = x * x
    t = jnp.tanh(scale * x * (1.0 + cubic * square))
    half = 0.5 * (1.0 + t)
    slope = half + (0.5 * scale) * x * (1.0 - t * t) * (1.0 + (3.0 * cubic) * square)
    return x * half, slope


def dot(left, right, left_dim=1, right_dim=0):
    return lax.dot_general(
        left, right, (((left_dim,), (right_dim,)), ((), ())), preferred_element_type=F32
    )


def round_kernel(
    n_pos,
    steps_ref,
    weights_ref,
    emb_ref,
    target_ref,
    gain_ref,
    model_ref,
    control_ref,
    own_ref,
    step_out,
    control_out,
    grad_out,
    packed,
    packed_in,
    model,
    current,
    g_rows,
    c_rows,
    corr,
    role_corr,
    sa_in,
    sa_out,
    sa_tiles,
    emb,
    target,
    normed,
    normed_t,
    act,
    slope_up,
    hidden,
    out_grad,
    out_grad_t,
    gate_grad,
    up_grad,
    term_out,
    term_own,
    term_in,
    tiles,
    sums_out,
    sums_in,
    final,
    final_in,
    local_sem,
    send_sem,
    recv_sem,
):
    parts, half, width = own_ref.shape
    rows = emb.shape[0]
    span = width // n_pos
    owner_span = span // 2
    n_other = n_pos - 1
    client = lax.axis_index("clients")
    x = lax.axis_index("fsdp")
    b = lax.rem(client, 2)
    p = client // 2
    home = b == x
    away = b != x
    role_client = 2 * p + x
    half_at = pl.multiple_of(b * half, half)
    other_at = pl.multiple_of((1 - b) * half, half)
    own_rows = pl.ds(half_at, half)
    other_rows = pl.ds(other_at, half)

    partner = {"clients": 2 * p + 1 - b, "fsdp": x}
    across = {"clients": client, "fsdp": 1 - x}
    swap = {"clients": 2 * p + 1 - b, "fsdp": 1 - x}

    def position(offset):
        return lax.rem(p + offset, n_pos)

    def plane(offset):
        return {"clients": 2 * position(offset) + b, "fsdp": x}

    def columns(pos):
        return pl.ds(pl.multiple_of(pos * span, span), span)

    counts = dict(
        pack=1, emb=1, target=1, cross=1, model=n_pos, g=n_pos, gfwd=n_pos, mfwd=n_pos,
        corr=parts, sain=parts, sa=n_pos, term0=parts, term1=parts, cur=parts, ret=parts,
        grad=n_pos * parts, sums=parts, final=1,
    )
    base = {}
    total = 0
    for name, count in counts.items():
        base[name] = total
        total += count

    def remote(src, dst, name, index, device):
        k = base[name] + index
        return pltpu.make_async_remote_copy(
            src_ref=src, dst_ref=dst, send_sem=send_sem.at[k], recv_sem=recv_sem.at[k],
            device_id=device, device_id_type=MESH,
        )

    def pack_copy():
        return remote(packed, packed_in, "pack", 0, partner)

    def emb_copy():
        return remote(
            emb_ref.at[pl.ds(rows, rows), :],
            emb.at[:, pl.ds(pl.multiple_of(x * half, half), half)],
            "emb", 0, across,
        )

    def target_copy():
        return remote(target_ref, target, "target", 0, swap)

    def model_window(row_window, pos):
        return model.at[:, row_window, columns(pos)]

    def cross_copy():
        window = model_window(own_rows, p)
        return remote(window, window, "cross", 0, across)

    def model_copy(d):
        window = model_window(own_rows, p)
        return remote(window, window, "model", d, plane(d))

    def model_arrival(d):
        window = model_window(own_rows, position(n_pos - d))
        return remote(window, window, "model", d, plane(d))

    def g_window(pos):
        return g_rows.at[:, :, columns(pos)]

    def g_copy(d):
        return remote(g_window(p), g_window(p), "g", d, plane(d))

    def g_arrival(d):
        pos = position(n_pos - d)
        return remote(g_window(pos), g_window(pos), "g", d, plane(d))

    def g_forward(d):
        pos = position(n_pos - d)
        return remote(g_window(pos), g_window(pos), "gfwd", d, partner)

    def model_forward(d):
        window = model_window(own_rows, position(n_pos - d))
        return remote(window, window, "mfwd", d, partner)

    def corr_copy(part):
        return remote(corr.at[part], role_corr.at[part], "corr", part, swap)

    def sain_copy(part):
        return remote(sa_out.at[part], sa_in.at[part], "sain", part, partner)

    def sa_copy(d):
        return remote(
            sa_out.at[:, :, columns(position(d))], sa_tiles.at[p], "sa", d, plane(d)
        )

    def sa_arrival(d):
        return remote(
            sa_out.at[:, :, columns(position(d))], sa_tiles.at[position(n_pos - d)],
            "sa", d, plane(d),
        )

    def term_copy(step, part):
        return remote(
            term_out.at[part], term_in.at[step, part], "term%d" % step, part, partner
        )

    def current_copy(part):
        window = current.at[part, own_rows, :]
        return remote(window, window, "cur", part, partner)

    def return_copy(part):
        return remote(role_corr.at[part], g_rows.at[part], "ret", part, swap)

    def grad_copy(d, part):
        return remote(
            role_corr.at[part, :, columns(position(d))], tiles.at[p, part],
            "grad", d * parts + part, plane(d),
        )

    def grad_arrival(d, part):
        pos = position(n_pos - d)
        return remote(
            role_corr.at[part, :, columns(position(d))], tiles.at[pos, part],
            "grad", d * parts + part, plane(d),
        )

    def sums_copy(part):
        return remote(sums_out.at[part], sums_in.at[part], "sums", part, across)

    def final_copy():
        return remote(final, final_in, "final", 0, partner)

    barrier = pltpu.get_barrier_semaphore()
    peers = [partner, across, swap] + [plane(d) for d in range(1, n_pos)]
    for peer in peers:
        pl.semaphore_signal(barrier, inc=1, device_id=peer, device_id_type=MESH)
    pl.semaphore_wait(barrier, len(peers))

    own_load = pltpu.make_async_copy(own_ref, c_rows, local_sem.at[0])
    emb_load = pltpu.make_async_copy(
        emb_ref.at[pl.ds(0, rows), :],
        emb.at[:, pl.ds(pl.multiple_of(x * half, half), half)],
        local_sem.at[1],
    )
    target_load = pltpu.make_async_copy(target_ref, target, local_sem.at[2])
    own_load.start()
    emb_load.start()

    packed[...] = jnp.concatenate(
        [model_ref[...].astype(BF), control_ref[...].astype(BF)], axis=-1
    )

    @pl.when(away)
    def _():
        pack_copy().start()
        emb_copy().start()
        target_copy().start()
        cross_copy().wait_recv()
        for d in range(1, n_pos):
            model_copy(d).start()

    @pl.when(home)
    def _():
        target_load.start()
        pack_copy().wait_recv()
        mine = packed[...]
        theirs = packed_in[...]
        first = jnp.where(b == 0, mine, theirs)
        second = jnp.where(b == 0, theirs, mine)
        model[:, own_rows, columns(p)] = jnp.concatenate(
            [first[:, :, :owner_span], second[:, :, :owner_span]], axis=-1
        )
        g_rows[:, :, columns(p)] = jnp.concatenate(
            [first[:, :, owner_span:], second[:, :, owner_span:]], axis=-1
        )
        cross_copy().start()
        for d in range(1, n_pos):
            g_copy(d).start()
        emb_copy().start()
        for d in range(1, n_pos):
            model_copy(d).start()
        g_forward(0).start()
        for d in range(1, n_pos):
            g_arrival(d).wait_recv()
            g_forward(d).start()

    model_forward(0).start()
    own_load.wait()

    @pl.when(away)
    def _():
        for d in range(n_pos):
            g_forward(d).wait_recv()

    own_steps = steps_ref[client]
    own_scale = (weights_ref[client] * own_steps).astype(F32)
    chunk = half // 6

    for part in range(parts):

        def correct(i, carry):
            at = pl.ds(pl.multiple_of(i * chunk, chunk), chunk)
            value = g_rows[part, at, :].astype(F32) - c_rows[part, at, :]
            rounded = value.astype(BF)
            corr[part, at, :] = rounded
            sa_out[part, at, :] = (own_scale * value).astype(BF)
            return carry

        lax.fori_loop(0, 6, correct, 0)

        @pl.when(away)
        def _():
            corr_copy(part).start()
            sain_copy(part).start()

    @pl.when(home)
    def _():
        for part in range(parts):

            def place(i, carry):
                at = pl.ds(pl.multiple_of(i * chunk, chunk), chunk)
                role_corr[part, at, :] = corr[part, at, :]
                return carry

            lax.fori_loop(0, 6, place, 0)
            sain_copy(part).wait_recv()

            def merge(i, carry):
                at = pl.ds(pl.multiple_of(i * chunk, chunk), chunk)
                sa_out[part, at, :] = (
                    sa_out[part, at, :].astype(F32) + sa_in[part, at, :].astype(F32)
                ).astype(BF)
                return carry

            lax.fori_loop(0, 6, merge, 0)
        for d in range(1, n_pos):
            sa_copy(d).start()

    emb_load.wait()
    emb_copy().wait_recv()
    widened = emb[...].astype(F32)
    inv_norm = lax.rsqrt(jnp.mean(widened * widened, axis=1, keepdims=True) + norm_eps)
    normed[...] = (widened * inv_norm * gain_ref[...]).astype(BF)
    depth = 2 * half
    for at in range(0, depth, 128):
        normed_t[at : at + 128, :] = normed[:, at : at + 128].T

    for d in range(1, n_pos):
        model_arrival(d).wait_recv()
        model_forward(d).start()
    for d in range(n_pos):
        model_forward(d).wait_recv()

    loss_scale = 1.0 / math.sqrt(2 * rows)
    n_tiles = width // TILE

    def tile_at(j):
        return pl.ds(pl.multiple_of(j * TILE, TILE), TILE)

    def half_product(left, left_rows, right, store):
        def product(j, carry):
            store(j, dot(left[left_rows, :], right[:, tile_at(j)]).astype(BF))
            return carry

        lax.fori_loop(0, n_tiles, product, 0)

    def local_step(step, weights, finish):
        def forward(j, carry):
            cols = tile_at(j)
            gate_act, slope = gelu_parts(dot(normed[...], weights[0, :, cols]))
            up_pre = dot(normed[...], weights[1, :, cols])
            act[:, cols] = gate_act
            slope_up[:, cols] = slope * up_pre
            hidden[:, cols] = (gate_act * up_pre).astype(BF)
            return carry

        lax.fori_loop(0, n_tiles, forward, 0)
        if step == 0:

            @pl.when(away)
            def _():
                target_copy().wait_recv()

            @pl.when(home)
            def _():
                target_load.wait()

        def project(j, carry):
            cols = tile_at(j)
            projected = dot(hidden[...], weights[2, cols, :], 1, 1)
            value = (
                (emb[:, cols].astype(F32) + projected - target[:, cols].astype(F32)) * loss_scale
            ).astype(BF)
            out_grad[:, cols] = value
            out_grad_t[cols, :] = value.T
            return carry

        lax.fori_loop(0, depth // TILE, project, 0)

        def term(part, left, right):
            def store_out(j, value):
                term_out[part, :, tile_at(j)] = value

            def store_own(j, value):
                term_own[part, :, tile_at(j)] = value

            if step > 0:
                term_copy(step - 1, part).wait_send()
            half_product(left, other_rows, right, store_out)
            term_copy(step, part).start()
            half_product(left, own_rows, right, store_own)

        term(2, out_grad_t, hidden)

        def backward(j, carry):
            cols = tile_at(j)
            hidden_grad = dot(out_grad[...], weights[2, :, cols])
            gate_grad[:, cols] = (hidden_grad * slope_up[:, cols]).astype(BF)
            up_grad[:, cols] = (hidden_grad * act[:, cols]).astype(BF)
            return carry

        lax.fori_loop(0, n_tiles, backward, 0)
        finish(2)
        term(0, normed_t, gate_grad)
        term(1, normed_t, up_grad)
        finish(0)
        finish(1)

    def update(part):
        term_copy(0, part).wait_recv()

        @pl.when(away)
        def _():
            corr_copy(part).wait_recv()

        def apply(i, carry):
            at = pl.ds(pl.multiple_of(i * chunk, chunk), chunk)
            model_at = pl.ds(pl.multiple_of(half_at + i * chunk, chunk), chunk)
            grads = term_own[part, at, :].astype(F32) + term_in[0, part, at, :].astype(F32)
            c_rows[part, at, :] = grads
            pseudo = grads + role_corr[part, at, :].astype(F32)
            current[part, model_at, :] = (
                model[part, model_at, :].astype(F32) - learning_rate * pseudo
            ).astype(BF)
            return carry

        lax.fori_loop(0, 6, apply, 0)
        current_copy(part).start()

    second = (steps_ref[role_client] > 1).astype(F32)

    def collect(part):
        term_copy(1, part).wait_recv()

        def apply(i, carry):
            at = pl.ds(pl.multiple_of(i * chunk, chunk), chunk)
            grads = term_own[part, at, :].astype(F32) + term_in[1, part, at, :].astype(F32)
            role_corr[part, at, :] = (c_rows[part, at, :] + second * grads).astype(BF)
            return carry

        lax.fori_loop(0, 6, apply, 0)

        @pl.when(away)
        def _():
            return_copy(part).start()

        @pl.when(home)
        def _():
            pltpu.make_async_copy(
                role_corr.at[part], grad_out.at[part], local_sem.at[3 + part]
            ).start()

        for d in range(1, n_pos):
            grad_copy(d, part).start()

    local_step(0, model, update)
    for part in range(parts):
        current_copy(part).wait_recv()
    local_step(1, current, collect)

    for part in (2, 0, 1):
        for d in range(1, n_pos):
            grad_arrival(d, part).wait_recv()
        weighted = jnp.zeros((half, span), F32)
        averaged = jnp.zeros((half, span), F32)
        for d in range(n_pos):
            pos = position(d)
            index = 2 * pos + x
            value = (
                role_corr[part, :, columns(p)] if d == 0 else tiles[pos, part]
            ).astype(F32)
            weight = weights_ref[index].astype(F32)
            taken = steps_ref[index].astype(F32)
            scaled = weight * value
            weighted += scaled
            averaged += scaled / taken
        final[part, 0] = weighted
        final[part, 1] = averaged

        @pl.when(away)
        def _():
            sums_out[part] = final[part].astype(BF)
            sums_copy(part).start()

    @pl.when(home)
    def _():
        for d in range(1, n_pos):
            sa_arrival(d).wait_recv()
        for part in (2, 0, 1):
            sums_copy(part).wait_recv()
            shift = sa_out[part, :, columns(p)].astype(F32)
            for d in range(1, n_pos):
                shift += sa_tiles[position(d), part].astype(F32)
            final[part, 0] = final[part, 0] + sums_in[part, 0].astype(F32) + shift
            final[part, 1] = final[part, 1] + sums_in[part, 1].astype(F32)
        final_copy().start()

    @pl.when(away)
    def _():
        final_copy().wait_recv()

    n_clients = 2 * n_pos
    weight_total = weights_ref[0]
    step_total = weights_ref[0] * steps_ref[0]
    for i in range(1, n_clients):
        weight_total += weights_ref[i]
        step_total += weights_ref[i] * steps_ref[i]
    weight_total = weight_total.astype(F32)
    step_total = step_total.astype(F32)

    def write(source):
        whole = source[...]
        own = jnp.where(b == 0, whole[..., :owner_span], whole[..., owner_span:])
        control = control_ref[...]
        lost = control - control.astype(BF).astype(F32)
        step_out[...] = (own[:, 0] + step_total * lost) / weight_total
        control_out[...] = own[:, 1] / weight_total

    @pl.when(home)
    def _():
        write(final)

    @pl.when(away)
    def _():
        write(final_in)

    @pl.when(away)
    def _():
        pack_copy().wait_send()
        target_copy().wait_send()
        for part in range(parts):
            corr_copy(part).wait_send()
            sain_copy(part).wait_send()
        for part in (2, 0, 1):
            return_copy(part).wait_recv()
            pltpu.make_async_copy(
                g_rows.at[part], grad_out.at[part], local_sem.at[3 + part]
            ).start()
        for part in range(parts):
            return_copy(part).wait_send()
            sums_copy(part).wait_send()

    @pl.when(home)
    def _():
        cross_copy().wait_send()
        for d in range(n_pos):
            g_forward(d).wait_send()
        for d in range(1, n_pos):
            g_copy(d).wait_send()
            sa_copy(d).wait_send()
        final_copy().wait_send()

    emb_copy().wait_send()
    for d in range(1, n_pos):
        model_copy(d).wait_send()
    for d in range(n_pos):
        model_forward(d).wait_send()
    for part in range(parts):
        term_copy(1, part).wait_send()
        current_copy(part).wait_send()
        for d in range(1, n_pos):
            grad_copy(d, part).wait_send()
    for part in range(parts):
        pltpu.make_async_copy(
            role_corr.at[part], grad_out.at[part], local_sem.at[3 + part]
        ).wait()


def paired_body(
    token_ids,
    target,
    embedding,
    norm_gain,
    global_model,
    global_control,
    client_control,
    local_steps,
    client_weight,
):
    n_clients = lax.axis_size("clients")
    n_pos = n_clients // 2
    parts, half, owner_span = global_model.shape
    width = owner_span * n_clients
    span = 2 * owner_span
    rows = token_ids.shape[1]
    depth = 2 * half
    pairs = [(c, f) for c in range(n_clients) for f in range(2)]
    to_role = [(c * 2 + f, (c - c % 2 + f) * 2 + c % 2) for c, f in pairs]
    to_across = [(c * 2 + f, (c - c % 2 + f) * 2 + 1 - c % 2) for c, f in pairs]
    ids = jnp.concatenate(
        [
            lax.ppermute(token_ids[0], ("clients", "fsdp"), to_role),
            lax.ppermute(token_ids[0], ("clients", "fsdp"), to_across),
        ]
    )
    emb_columns = embedding.at[ids].get(mode="promise_in_bounds")

    n_sem = 5 + 5 * n_pos + 7 * parts + n_pos * parts
    vmem = pltpu.VMEM
    scratch = [
        vmem((parts, half, span), BF),
        vmem((parts, half, span), BF),
        vmem((parts, depth, width), BF),
        vmem((parts, depth, width), BF),
        vmem((parts, half, width), BF),
        vmem((parts, half, width), F32),
        vmem((parts, half, width), BF),
        vmem((parts, half, width), BF),
        vmem((parts, half, width), BF),
        vmem((parts, half, width), BF),
        vmem((n_pos, parts, half, span), BF),
        vmem((rows, depth), BF),
        vmem((rows, depth), BF),
        vmem((rows, depth), BF),
        vmem((depth, rows), BF),
        vmem((rows, width), F32),
        vmem((rows, width), F32),
        vmem((rows, width), BF),
        vmem((rows, depth), BF),
        vmem((depth, rows), BF),
        vmem((rows, width), BF),
        vmem((rows, width), BF),
        vmem((parts, half, width), BF),
        vmem((parts, half, width), BF),
        vmem((2, parts, half, width), BF),
        vmem((n_pos, parts, half, span), BF),
        vmem((parts, 2, half, span), BF),
        vmem((parts, 2, half, span), BF),
        vmem((parts, 2, half, span), F32),
        vmem((parts, 2, half, span), F32),
        pltpu.SemaphoreType.DMA((3 + parts,)),
        pltpu.SemaphoreType.DMA((n_sem,)),
        pltpu.SemaphoreType.DMA((n_sem,)),
    ]
    smem = pl.BlockSpec(memory_space=pltpu.SMEM)
    anywhere = pl.BlockSpec(memory_space=pl.ANY)
    inside = pl.BlockSpec(memory_space=pltpu.VMEM)
    step_sum, control_sum, grad_rows = pl.pallas_call(
        functools.partial(round_kernel, n_pos),
        out_shape=(
            jax.ShapeDtypeStruct((parts, half, owner_span), F32),
            jax.ShapeDtypeStruct((parts, half, owner_span), F32),
            jax.ShapeDtypeStruct((parts, half, width), BF),
        ),
        in_specs=[smem, smem, anywhere, anywhere, inside, inside, inside, anywhere],
        out_specs=(inside, inside, anywhere),
        scratch_shapes=scratch,
        compiler_params=pltpu.CompilerParams(
            collective_id=0, has_side_effects=True, vmem_limit_bytes=67043328
        ),
    )(
        local_steps,
        client_weight,
        emb_columns,
        target[0],
        norm_gain[None, :],
        global_model,
        global_control,
        client_control[0],
    )
    slots = jnp.arange(n_clients)
    own_steps = jnp.sum(jnp.where(slots == lax.axis_index("clients"), local_steps, 0))
    update = grad_rows.astype(F32) / own_steps.astype(F32)
    return (step_sum, control_sum, update[None])


def solution(mesh):
    placed = (
        P("clients", "fsdp"),
        P("clients", "fsdp", None),
        P(None, "fsdp"),
        P(),
        P(None, "fsdp", "clients"),
        P(None, "fsdp", "clients"),
        P("clients", None, "fsdp", None),
        P(),
        P(),
    )
    paired = mesh.shape["fsdp"] == 2 and mesh.shape["clients"] % 2 == 0
    return jax.shard_map(
        paired_body if paired else general_body,
        mesh=mesh,
        in_specs=placed,
        out_specs=(
            P(None, "fsdp", "clients"),
            P(None, "fsdp", "clients"),
            P("clients", None, "fsdp", None),
        ),
        check_vma=False,
    )
```

profile of v0, /device:TPU:29, one launch (start us, length us, event | category | flops | bytes accessed | tf_op | source)
XLA Modules:
  0.0 222.5 jit_solution(4007872537280677761)
XLA Ops:
  0.6 0.7 reduce
  1.3 0.7 collective-permute-start.1
  2.0 3.0 %collective-permute-start = (s32[640]{0:T(1024)S(1)}, s32[640]{0:T(1024)S(1)}, u32[]{:S(2)}, u32[]{:S(2)}) collective-permute-start(s32[640]{0:T(1024)S(1)} %reduce), channel_id=1, source_target_pairs={{0,0},{1,2},{2,1},{3,3},{4,4},{5,6},{6,5},{7,7},{8,8},{9,10},{10,9... | collective-permute-start | bytes 7688 | tf_op jit(solution)/shard_map/ppermute | solution.py:762
  5.1 1.3 fusion.1
  7.0 1.3 broadcast_in_dim.11.gain_ref
  8.3 2.0 copy.16.model_ref
  10.3 2.0 copy.17.control_ref
  12.3 0.0 collective-permute-done
  12.3 0.0 collective-permute-done.1
  12.4 10.6 %gather_fusion = bf16[1280,384]{1,0:T(8,128)(2,1)} fusion(bf16[16384,384]{1,0:T(8,128)(2,1)} %param.11, s32[2048]{0:T(1024)S(1)} %pad_clamp_fusion), kind=kCustom, calls=%fused_computation | custom fusion | bytes 1971200 | tf_op jit(solution)/shard_map/gather | solution.py:766
  23.0 191.0 %shard_map.112 = (f32[3,384,64]{2,1,0:T(8,128)}, f32[3,384,64]{2,1,0:T(8,128)}, bf16[3,384,1024]{2,1,0:T(8,128)(2,1)}) custom-call(s32[16]{0:T(128)} %steps_ref.1, s32[16]{0:T(128)} %weights_ref.1, bf16[1280,384]{1,0:T(8,128)(2,1)} %gather_fusion, bf16[640,768]{1,0:T(8,128)(2,1)} %bitcast.5, f32[1,768]{1,0:T(1,128)} %broadcast_in_dim.11.gain_ref, ...), custom_call_target="tpu_custom_call" | custom-call | tf_op jit(solution)/shard_map/pallas_call | solution.py:808
  214.0 2.0 copy.18
  216.0 2.0 copy.19
  218.0 4.5 %divide_bitcast_fusion = f32[1,3,384,1024]{3,2,1,0:T(8,128)} fusion(bf16[3,384,1024]{2,1,0:T(8,128)(2,1)} %get-tuple-element.8, f32[]{:T(128)S(6)} %convert_element_type.7), kind=kLoop, calls=%fused_computation.1 | loop fusion | flops 2359296 | bytes 7077892 | tf_op jit(solution)/shard_map/broadcast_in_dim | solution.py:834
  (4 shorter events, 0.0 us)
Async XLA Ops:
  1.3 11.0 %collective-permute-start.1 = (s32[640]{0:T(1024)S(1)}, s32[640]{0:T(1024)S(1)}, u32[]{:S(2)}, u32[]{:S(2)}) collective-permute-start(s32[640]{0:T(1024)S(1)} %reduce), channel_id=1, source_target_pairs={{0,1},{1,3},{2,0},{3,2},{4,5},{5,7},{6,4},{7,6},{8,9},{9,11},{10,8... | collective-permute-start | bytes 7688 | tf_op jit(solution)/shard_map/ppermute | solution.py:763
  2.0 10.3 %collective-permute-start = (s32[640]{0:T(1024)S(1)}, s32[640]{0:T(1024)S(1)}, u32[]{:S(2)}, u32[]{:S(2)}) collective-permute-start(s32[640]{0:T(1024)S(1)} %reduce), channel_id=1, source_target_pairs={{0,0},{1,2},{2,1},{3,3},{4,4},{5,6},{6,5},{7,7},{8,8},{9,10},{10,9... | collective-permute-start | bytes 7688 | tf_op jit(solution)/shard_map/ppermute | solution.py:762
where the time goes:
time: 223 us
  Pallas kernels  191 us (86%)
  local copies, waits for them, and re-layouts  19.9 us (9%)
  other arithmetic  6.56 us (3%)
  starting transfers between devices  3.71 us (2%)
    pallas_call x1, Pallas kernels, paired_body(): pl.pallas_call(functools.partial(round_kernel, n_pos), out_shape=(jax.Sha...  191 us
    gather x1, local copies, waits for them, and re-layouts, paired_body(): emb_columns = embedding.at[ids].get(mode='promise_in_bounds')  10.6 us
    unnamed x5, local copies, waits for them, and re-layouts  8.03 us
    broadcast_in_dim x1, other arithmetic, paired_body(): return (step_sum, control_sum, update[None])  4.54 us
  transfers between devices with their start and end apart: 2, of which 0 were waited for; matrix products, arithmetic and copies ran while one was open for 3% of the time, Pallas kernels for 0%

commit v1 on v0

--- a/solution.py
+++ b/solution.py
@@ -192,7 +192,7 @@
 
 
 def round_kernel(
-    n_pos,
+    n_z,
     steps_ref,
     weights_ref,
     emb_ref,
@@ -205,16 +205,12 @@
     control_out,
     grad_out,
     packed,
-    packed_in,
     model,
     current,
     g_rows,
     c_rows,
     corr,
     role_corr,
-    sa_in,
-    sa_out,
-    sa_tiles,
     emb,
     target,
     normed,
@@ -229,9 +225,11 @@
     term_out,
     term_own,
     term_in,
-    tiles,
-    sums_out,
-    sums_in,
+    share_in,
+    kept,
+    y_out,
+    y_in,
+    z_in,
     final,
     final_in,
     local_sem,
@@ -240,13 +238,18 @@
 ):
     parts, half, width = own_ref.shape
     rows = emb.shape[0]
+    depth = 2 * half
+    n_pos = 2 * n_z
     span = width // n_pos
     owner_span = span // 2
-    n_other = n_pos - 1
+    sub = kept.shape[2]
+    n_sub = half // sub
     client = lax.axis_index("clients")
     x = lax.axis_index("fsdp")
     b = lax.rem(client, 2)
     p = client // 2
+    y = lax.rem(p, 2)
+    z = p // 2
     home = b == x
     away = b != x
     role_client = 2 * p + x
@@ -254,24 +257,32 @@
     other_at = pl.multiple_of((1 - b) * half, half)
     own_rows = pl.ds(half_at, half)
     other_rows = pl.ds(other_at, half)
+    owner_at = pl.multiple_of(b * owner_span, owner_span)
 
     partner = {"clients": 2 * p + 1 - b, "fsdp": x}
     across = {"clients": client, "fsdp": 1 - x}
     swap = {"clients": 2 * p + 1 - b, "fsdp": 1 - x}
-
-    def position(offset):
-        return lax.rem(p + offset, n_pos)
-
-    def plane(offset):
-        return {"clients": 2 * position(offset) + b, "fsdp": x}
+    beside = {"clients": 2 * (2 * z + 1 - y) + b, "fsdp": x}
+
+    def along(d):
+        return {"clients": 2 * (2 * lax.rem(z + d, n_z) + y) + b, "fsdp": x}
+
+    def behind(d):
+        return lax.rem(z + n_z - d, n_z)
+
+    def position(line, d):
+        row = y if line == 0 else 1 - y
+        return 2 * behind(d) + row
 
     def columns(pos):
         return pl.ds(pl.multiple_of(pos * span, span), span)
 
+    n_chunks = parts * n_sub
+    groups = ((0, parts - 1), (parts - 1, 1))
     counts = dict(
-        pack=1, emb=1, target=1, cross=1, model=n_pos, g=n_pos, gfwd=n_pos, mfwd=n_pos,
-        corr=parts, sain=parts, sa=n_pos, term0=parts, term1=parts, cur=parts, ret=parts,
-        grad=n_pos * parts, sums=parts, final=1,
+        pack=1, emb=1, target=1, cross=2, gz=n_z, gy=n_z, gp=n_pos, mz=2 * n_z, my=2 * n_z,
+        mp=2 * n_pos, corr=parts, term0=parts, term1=parts, cur=parts, ret=n_chunks,
+        share=n_chunks, ry=n_chunks, rz=n_chunks * n_z, final=1,
     )
     base = {}
     total = 0
@@ -287,7 +298,8 @@
         )
 
     def pack_copy():
-        return remote(packed, packed_in, "pack", 0, partner)
+        window = packed.at[:, :, pl.ds(owner_at, owner_span), :]
+        return remote(window, window, "pack", 0, partner)
 
     def emb_copy():
         return remote(
@@ -299,55 +311,43 @@
     def target_copy():
         return remote(target_ref, target, "target", 0, swap)
 
-    def model_window(row_window, pos):
-        return model.at[:, row_window, columns(pos)]
-
-    def cross_copy():
-        window = model_window(own_rows, p)
-        return remote(window, window, "cross", 0, across)
-
-    def model_copy(d):
-        window = model_window(own_rows, p)
-        return remote(window, window, "model", d, plane(d))
-
-    def model_arrival(d):
-        window = model_window(own_rows, position(n_pos - d))
-        return remote(window, window, "model", d, plane(d))
-
     def g_window(pos):
         return g_rows.at[:, :, columns(pos)]
 
-    def g_copy(d):
-        return remote(g_window(p), g_window(p), "g", d, plane(d))
-
-    def g_arrival(d):
-        pos = position(n_pos - d)
-        return remote(g_window(pos), g_window(pos), "g", d, plane(d))
-
-    def g_forward(d):
-        pos = position(n_pos - d)
-        return remote(g_window(pos), g_window(pos), "gfwd", d, partner)
-
-    def model_forward(d):
-        window = model_window(own_rows, position(n_pos - d))
-        return remote(window, window, "mfwd", d, partner)
+    def model_window(group, pos):
+        first, count = groups[group]
+        return model.at[pl.ds(first, count), own_rows, columns(pos)]
+
+    def g_along(d, source):
+        window = g_window(source)
+        return remote(window, window, "gz", d, along(d))
+
+    def g_beside(d, source):
+        window = g_window(source)
+        return remote(window, window, "gy", d, beside)
+
+    def g_partner(line, d):
+        window = g_window(position(line, d))
+        return remote(window, window, "gp", line * n_z + d, partner)
+
+    def cross_copy(group):
+        window = model_window(group, p)
+        return remote(window, window, "cross", group, across)
+
+    def model_along(group, d, source):
+        window = model_window(group, source)
+        return remote(window, window, "mz", group * n_z + d, along(d))
+
+    def model_beside(group, d, source):
+        window = model_window(group, source)
+        return remote(window, window, "my", group * n_z + d, beside)
+
+    def model_partner(group, line, d):
+        window = model_window(group, position(line, d))
+        return remote(window, window, "mp", group * n_pos + line * n_z + d, partner)
 
     def corr_copy(part):
         return remote(corr.at[part], role_corr.at[part], "corr", part, swap)
-
-    def sain_copy(part):
-        return remote(sa_out.at[part], sa_in.at[part], "sain", part, partner)
-
-    def sa_copy(d):
-        return remote(
-            sa_out.at[:, :, columns(position(d))], sa_tiles.at[p], "sa", d, plane(d)
-        )
-
-    def sa_arrival(d):
-        return remote(
-            sa_out.at[:, :, columns(position(d))], sa_tiles.at[position(n_pos - d)],
-            "sa", d, plane(d),
-        )
 
     def term_copy(step, part):
         return remote(
@@ -358,33 +358,47 @@
         window = current.at[part, own_rows, :]
         return remote(window, window, "cur", part, partner)
 
-    def return_copy(part):
-        return remote(role_corr.at[part], g_rows.at[part], "ret", part, swap)
-
-    def grad_copy(d, part):
+    def sub_rows(s):
+        return pl.ds(s * sub, sub)
+
+    def return_copy(part, s):
         return remote(
-            role_corr.at[part, :, columns(position(d))], tiles.at[p, part],
-            "grad", d * parts + part, plane(d),
-        )
-
-    def grad_arrival(d, part):
-        pos = position(n_pos - d)
+            role_corr.at[part, sub_rows(s), :], g_rows.at[part, sub_rows(s), :],
+            "ret", part * n_sub + s, swap,
+        )
+
+    def share_copy(part, s):
         return remote(
-            role_corr.at[part, :, columns(position(d))], tiles.at[pos, part],
-            "grad", d * parts + part, plane(d),
-        )
-
-    def sums_copy(part):
-        return remote(sums_out.at[part], sums_in.at[part], "sums", part, across)
+            term_out.at[part, sub_rows(s), :], share_in.at[part, sub_rows(s), :],
+            "share", part * n_sub + s, partner,
+        )
+
+    def y_copy(k):
+        return remote(y_out.at[k], y_in.at[k], "ry", k, beside)
+
+    def z_copy(k, d):
+        return remote(
+            kept.at[k, lax.rem(z + d, n_z)], z_in.at[k, d], "rz", k * n_z + d, along(d)
+        )
 
     def final_copy():
-        return remote(final, final_in, "final", 0, partner)
+        return remote(
+            final.at[:, pl.ds(pl.multiple_of((1 - b) * owner_span, owner_span), owner_span), :],
+            final_in, "final", 0, partner,
+        )
+
+    def grad_store(part, s):
+        return pltpu.make_async_copy(
+            term_in.at[0, part, sub_rows(s), :], grad_out.at[part, sub_rows(s), :],
+            local_sem.at[3 + part * n_sub + s],
+        )
 
     barrier = pltpu.get_barrier_semaphore()
-    peers = [partner, across, swap] + [plane(d) for d in range(1, n_pos)]
-    for peer in peers:
+    for peer in [partner, across, swap, beside]:
         pl.semaphore_signal(barrier, inc=1, device_id=peer, device_id_type=MESH)
-    pl.semaphore_wait(barrier, len(peers))
+    for d in range(1, n_z):
+        pl.semaphore_signal(barrier, inc=1, device_id=along(d), device_id_type=MESH)
+    pl.semaphore_wait(barrier, 3 + n_z)
 
     own_load = pltpu.make_async_copy(own_ref, c_rows, local_sem.at[0])
     emb_load = pltpu.make_async_copy(
@@ -393,67 +407,80 @@
         local_sem.at[1],
     )
     target_load = pltpu.make_async_copy(target_ref, target, local_sem.at[2])
-    own_load.start()
-    emb_load.start()
-
-    packed[...] = jnp.concatenate(
-        [model_ref[...].astype(BF), control_ref[...].astype(BF)], axis=-1
-    )
+
+    packed[0, :, pl.ds(owner_at, owner_span), :] = model_ref[...].astype(BF)
+    packed[1, :, pl.ds(owner_at, owner_span), :] = control_ref[...].astype(BF)
 
     @pl.when(away)
     def _():
         pack_copy().start()
         emb_copy().start()
         target_copy().start()
-        cross_copy().wait_recv()
-        for d in range(1, n_pos):
-            model_copy(d).start()
+
+    own_load.start()
+    emb_load.start()
 
     @pl.when(home)
     def _():
         target_load.start()
-        pack_copy().wait_recv()
-        mine = packed[...]
-        theirs = packed_in[...]
-        first = jnp.where(b == 0, mine, theirs)
-        second = jnp.where(b == 0, theirs, mine)
-        model[:, own_rows, columns(p)] = jnp.concatenate(
-            [first[:, :, :owner_span], second[:, :, :owner_span]], axis=-1
-        )
-        g_rows[:, :, columns(p)] = jnp.concatenate(
-            [first[:, :, owner_span:], second[:, :, owner_span:]], axis=-1
-        )
-        cross_copy().start()
-        for d in range(1, n_pos):
-            g_copy(d).start()
+        partner_pack = packed.at[
+            :, :, pl.ds(pl.multiple_of((1 - b) * owner_span, owner_span), owner_span), :
+        ]
+        remote(partner_pack, partner_pack, "pack", 0, partner).wait_recv()
+        for part in range(parts):
+            g_rows[part, :, columns(p)] = packed[1, part].T
+        for d in range(1, n_z):
+            g_along(d, p).start()
+        g_beside(0, p).start()
+        for part in range(parts):
+            model[part, own_rows, columns(p)] = packed[0, part].T
+        for group in range(2):
+            cross_copy(group).start()
         emb_copy().start()
-        for d in range(1, n_pos):
-            model_copy(d).start()
-        g_forward(0).start()
-        for d in range(1, n_pos):
-            g_arrival(d).wait_recv()
-            g_forward(d).start()
-
-    model_forward(0).start()
-    own_load.wait()
+        for group in range(2):
+            for d in range(1, n_z):
+                model_along(group, d, p).start()
+        g_partner(0, 0).start()
+        for d in range(1, n_z):
+            g_along(d, position(0, d)).wait_recv()
+            g_beside(d, position(0, d)).start()
+            g_partner(0, d).start()
+        model_beside(0, 0, p).start()
+        model_beside(1, 0, p).start()
+        for d in range(n_z):
+            g_beside(d, position(1, d)).wait_recv()
+            g_partner(1, d).start()
 
     @pl.when(away)
     def _():
-        for d in range(n_pos):
-            g_forward(d).wait_recv()
-
-    own_steps = steps_ref[client]
-    own_scale = (weights_ref[client] * own_steps).astype(F32)
+        for group in range(2):
+            cross_copy(group).wait_recv()
+            for d in range(1, n_z):
+                model_along(group, d, p).start()
+            model_beside(group, 0, p).start()
+
+    for group in range(2):
+        model_partner(group, 0, 0).start()
+    own_load.wait()
+
+    @pl.when(away)
+    def _():
+        for line in range(2):
+            for d in range(n_z):
+                g_partner(line, d).wait_recv()
+
     chunk = half // 6
-
     for part in range(parts):
 
         def correct(i, carry):
             at = pl.ds(pl.multiple_of(i * chunk, chunk), chunk)
-            value = g_rows[part, at, :].astype(F32) - c_rows[part, at, :]
-            rounded = value.astype(BF)
-            corr[part, at, :] = rounded
-            sa_out[part, at, :] = (own_scale * value).astype(BF)
+            value = (g_rows[part, at, :].astype(F32) - c_rows[part, at, :]).astype(BF)
+            corr[part, at, :] = value
+
+            @pl.when(home)
+            def _():
+                role_corr[part, at, :] = value
+
             return carry
 
         lax.fori_loop(0, 6, correct, 0)
@@ -461,45 +488,38 @@
         @pl.when(away)
         def _():
             corr_copy(part).start()
-            sain_copy(part).start()
-
-    @pl.when(home)
-    def _():
-        for part in range(parts):
-
-            def place(i, carry):
-                at = pl.ds(pl.multiple_of(i * chunk, chunk), chunk)
-                role_corr[part, at, :] = corr[part, at, :]
-                return carry
-
-            lax.fori_loop(0, 6, place, 0)
-            sain_copy(part).wait_recv()
-
-            def merge(i, carry):
-                at = pl.ds(pl.multiple_of(i * chunk, chunk), chunk)
-                sa_out[part, at, :] = (
-                    sa_out[part, at, :].astype(F32) + sa_in[part, at, :].astype(F32)
-                ).astype(BF)
-                return carry
-
-            lax.fori_loop(0, 6, merge, 0)
-        for d in range(1, n_pos):
-            sa_copy(d).start()
 
     emb_load.wait()
     emb_copy().wait_recv()
-    widened = emb[...].astype(F32)
-    inv_norm = lax.rsqrt(jnp.mean(widened * widened, axis=1, keepdims=True) + norm_eps)
-    normed[...] = (widened * inv_norm * gain_ref[...]).astype(BF)
-    depth = 2 * half
-    for at in range(0, depth, 128):
-        normed_t[at : at + 128, :] = normed[:, at : at + 128].T
-
-    for d in range(1, n_pos):
-        model_arrival(d).wait_recv()
-        model_forward(d).start()
-    for d in range(n_pos):
-        model_forward(d).wait_recv()
+    block = rows // 5
+
+    def normalise(i, carry):
+        at = pl.ds(pl.multiple_of(i * block, block), block)
+        widened = emb[at, :].astype(F32)
+        inv_norm = lax.rsqrt(jnp.mean(widened * widened, axis=1, keepdims=True) + norm_eps)
+        value = (widened * inv_norm * gain_ref[...]).astype(BF)
+        normed[at, :] = value
+        normed_t[:, at] = value.T
+        return carry
+
+    lax.fori_loop(0, 5, normalise, 0)
+
+    def relay(group, d):
+        model_along(group, d, position(0, d)).wait_recv()
+        model_beside(group, d, position(0, d)).start()
+        model_partner(group, 0, d).start()
+
+    def settle(group):
+        for d in range(n_z):
+            model_beside(group, d, position(1, d)).wait_recv()
+            model_partner(group, 1, d).start()
+        for line in range(2):
+            for d in range(n_z):
+                model_partner(group, line, d).wait_recv()
+
+    for d in range(1, n_z):
+        relay(0, d)
+    settle(0)
 
     loss_scale = 1.0 / math.sqrt(2 * rows)
     n_tiles = width // TILE
@@ -526,6 +546,9 @@
 
         lax.fori_loop(0, n_tiles, forward, 0)
         if step == 0:
+            for d in range(1, n_z):
+                relay(1, d)
+            settle(1)
 
             @pl.when(away)
             def _():
@@ -601,98 +624,106 @@
 
     def collect(part):
         term_copy(1, part).wait_recv()
-
-        def apply(i, carry):
-            at = pl.ds(pl.multiple_of(i * chunk, chunk), chunk)
+        for s in range(n_sub):
+            at = sub_rows(s)
             grads = term_own[part, at, :].astype(F32) + term_in[1, part, at, :].astype(F32)
             role_corr[part, at, :] = (c_rows[part, at, :] + second * grads).astype(BF)
-            return carry
-
-        lax.fori_loop(0, 6, apply, 0)
-
-        @pl.when(away)
-        def _():
-            return_copy(part).start()
-
-        @pl.when(home)
-        def _():
-            pltpu.make_async_copy(
-                role_corr.at[part], grad_out.at[part], local_sem.at[3 + part]
-            ).start()
-
-        for d in range(1, n_pos):
-            grad_copy(d, part).start()
+
+            @pl.when(away)
+            def _():
+                return_copy(part, s).start()
 
     local_step(0, model, update)
     for part in range(parts):
         current_copy(part).wait_recv()
     local_step(1, current, collect)
 
-    for part in (2, 0, 1):
-        for d in range(1, n_pos):
-            grad_arrival(d, part).wait_recv()
-        weighted = jnp.zeros((half, span), F32)
-        averaged = jnp.zeros((half, span), F32)
-        for d in range(n_pos):
-            pos = position(d)
-            index = 2 * pos + x
-            value = (
-                role_corr[part, :, columns(p)] if d == 0 else tiles[pos, part]
-            ).astype(F32)
-            weight = weights_ref[index].astype(F32)
-            taken = steps_ref[index].astype(F32)
-            scaled = weight * value
-            weighted += scaled
-            averaged += scaled / taken
-        final[part, 0] = weighted
-        final[part, 1] = averaged
+    weight = weights_ref[client].astype(F32)
+    taken = steps_ref[client].astype(F32)
+    inverse = 1.0 / taken
+    order = [(part, s) for part in (2, 0, 1) for s in range(n_sub)]
+
+    def share(part, s):
+        at = sub_rows(s)
+        if s == 0:
+            term_copy(1, part).wait_send()
+
+        def spread(source):
+            value = source[part, at, :].astype(F32)
+            averaged = inverse * value
+            summed = value + taken * corr[part, at, :].astype(F32)
+            term_in[0, part, at, :] = averaged.astype(BF)
+            mine = jnp.where(b == 0, summed, averaged)
+            theirs = jnp.where(b == 0, averaged, summed)
+            term_own[part, at, :] = (weight * mine).astype(BF)
+            term_out[part, at, :] = (weight * theirs).astype(BF)
+
+        @pl.when(home)
+        def _():
+            spread(role_corr)
 
         @pl.when(away)
         def _():
-            sums_out[part] = final[part].astype(BF)
-            sums_copy(part).start()
-
-    @pl.when(home)
-    def _():
-        for d in range(1, n_pos):
-            sa_arrival(d).wait_recv()
-        for part in (2, 0, 1):
-            sums_copy(part).wait_recv()
-            shift = sa_out[part, :, columns(p)].astype(F32)
-            for d in range(1, n_pos):
-                shift += sa_tiles[position(d), part].astype(F32)
-            final[part, 0] = final[part, 0] + sums_in[part, 0].astype(F32) + shift
-            final[part, 1] = final[part, 1] + sums_in[part, 1].astype(F32)
-        final_copy().start()
-
-    @pl.when(away)
-    def _():
-        final_copy().wait_recv()
-
-    n_clients = 2 * n_pos
+            return_copy(part, s).wait_recv()
+            spread(g_rows)
+
+        share_copy(part, s).start()
+        grad_store(part, s).start()
+
+    def split(k):
+        part, s = order[k]
+        at = sub_rows(s)
+        share_copy(part, s).wait_recv()
+        for row in range(n_z):
+            for line in range(2):
+                cols = columns(2 * row + (y if line == 0 else 1 - y))
+                value = (
+                    term_own[part, at, cols].astype(F32) + share_in[part, at, cols].astype(F32)
+                ).astype(BF)
+                if line == 0:
+                    kept[k, row] = value
+                else:
+                    y_out[k, row] = value
+        y_copy(k).start()
+
+    def spread_z(k):
+        y_copy(k).wait_recv()
+        kept[k] = (kept[k].astype(F32) + y_in[k].astype(F32)).astype(BF)
+        for d in range(1, n_z):
+            z_copy(k, d).start()
+
+    def gather_z(k):
+        part, s = order[k]
+        value = kept[k, z].astype(F32)
+        for d in range(1, n_z):
+            z_copy(k, d).wait_recv()
+            value += z_in[k, d].astype(F32)
+        final[part, :, sub_rows(s)] = value.T
+
+    for k in range(n_chunks + 2):
+        if k < n_chunks:
+            share(*order[k])
+            split(k)
+        if 0 <= k - 1 < n_chunks:
+            spread_z(k - 1)
+        if 0 <= k - 2:
+            gather_z(k - 2)
+    final_copy().start()
+
     weight_total = weights_ref[0]
     step_total = weights_ref[0] * steps_ref[0]
-    for i in range(1, n_clients):
+    for i in range(1, 2 * n_pos):
         weight_total += weights_ref[i]
         step_total += weights_ref[i] * steps_ref[i]
     weight_total = weight_total.astype(F32)
     step_total = step_total.astype(F32)
-
-    def write(source):
-        whole = source[...]
-        own = jnp.where(b == 0, whole[..., :owner_span], whole[..., owner_span:])
-        control = control_ref[...]
-        lost = control - control.astype(BF).astype(F32)
-        step_out[...] = (own[:, 0] + step_total * lost) / weight_total
-        control_out[...] = own[:, 1] / weight_total
-
-    @pl.when(home)
-    def _():
-        write(final)
-
-    @pl.when(away)
-    def _():
-        write(final_in)
+    control = control_ref[...]
+    lost = step_total * (control - control.astype(BF).astype(F32))
+    final_copy().wait_recv()
+    mine = final[:, pl.ds(owner_at, owner_span), :]
+    theirs = final_in[...]
+    step_out[...] = (jnp.where(b == 0, mine, theirs) + lost) / weight_total
+    control_out[...] = jnp.where(b == 0, theirs, mine) / weight_total
 
     @pl.when(away)
     def _():
@@ -700,40 +731,38 @@
         target_copy().wait_send()
         for part in range(parts):
             corr_copy(part).wait_send()
-            sain_copy(part).wait_send()
-        for part in (2, 0, 1):
-            return_copy(part).wait_recv()
-            pltpu.make_async_copy(
-                g_rows.at[part], grad_out.at[part], local_sem.at[3 + part]
-            ).start()
-        for part in range(parts):
-            return_copy(part).wait_send()
-            sums_copy(part).wait_send()
+            for s in range(n_sub):
+                return_copy(part, s).wait_send()
 
     @pl.when(home)
     def _():
-        cross_copy().wait_send()
-        for d in range(n_pos):
-            g_forward(d).wait_send()
-        for d in range(1, n_pos):
-            g_copy(d).wait_send()
-            sa_copy(d).wait_send()
-        final_copy().wait_send()
+        for group in range(2):
+            cross_copy(group).wait_send()
+        for d in range(n_z):
+            if d > 0:
+                g_along(d, p).wait_send()
+            g_beside(d, position(0, d)).wait_send()
+            for line in range(2):
+                g_partner(line, d).wait_send()
 
     emb_copy().wait_send()
-    for d in range(1, n_pos):
-        model_copy(d).wait_send()
-    for d in range(n_pos):
-        model_forward(d).wait_send()
+    for group in range(2):
+        for d in range(n_z):
+            if d > 0:
+                model_along(group, d, p).wait_send()
+            model_beside(group, d, position(0, d)).wait_send()
+            for line in range(2):
+                model_partner(group, line, d).wait_send()
     for part in range(parts):
-        term_copy(1, part).wait_send()
         current_copy(part).wait_send()
-        for d in range(1, n_pos):
-            grad_copy(d, part).wait_send()
-    for part in range(parts):
-        pltpu.make_async_copy(
-            role_corr.at[part], grad_out.at[part], local_sem.at[3 + part]
-        ).wait()
+        for s in range(n_sub):
+            share_copy(part, s).wait_send()
+            grad_store(part, s).wait()
+    for k in range(n_chunks):
+        y_copy(k).wait_send()
+        for d in range(1, n_z):
+            z_copy(k, d).wait_send()
+    final_copy().wait_send()
 
 
 def paired_body(
@@ -749,11 +778,14 @@
 ):
     n_clients = lax.axis_size("clients")
     n_pos = n_clients // 2
+    n_z = n_pos // 2
     parts, half, owner_span = global_model.shape
     width = owner_span * n_clients
     span = 2 * owner_span
     rows = token_ids.shape[1]
     depth = 2 * half
+    sub = 128
+    n_chunks = parts * (half // sub)
     pairs = [(c, f) for c in range(n_clients) for f in range(2)]
     to_role = [(c * 2 + f, (c - c % 2 + f) * 2 + c % 2) for c, f in pairs]
     to_across = [(c * 2 + f, (c - c % 2 + f) * 2 + 1 - c % 2) for c, f in pairs]
@@ -765,20 +797,16 @@
     )
     emb_columns = embedding.at[ids].get(mode="promise_in_bounds")
 
-    n_sem = 5 + 5 * n_pos + 7 * parts + n_pos * parts
+    n_sem = 6 + 6 * n_z + 3 * n_pos + 4 * parts + n_chunks * (3 + n_z)
     vmem = pltpu.VMEM
     scratch = [
-        vmem((parts, half, span), BF),
-        vmem((parts, half, span), BF),
+        vmem((2, parts, span, half), BF),
         vmem((parts, depth, width), BF),
         vmem((parts, depth, width), BF),
         vmem((parts, half, width), BF),
         vmem((parts, half, width), F32),
         vmem((parts, half, width), BF),
         vmem((parts, half, width), BF),
-        vmem((parts, half, width), BF),
-        vmem((parts, half, width), BF),
-        vmem((n_pos, parts, half, span), BF),
         vmem((rows, depth), BF),
         vmem((rows, depth), BF),
         vmem((rows, depth), BF),
@@ -793,12 +821,14 @@
         vmem((parts, half, width), BF),
         vmem((parts, half, width), BF),
         vmem((2, parts, half, width), BF),
-        vmem((n_pos, parts, half, span), BF),
-        vmem((parts, 2, half, span), BF),
-        vmem((parts, 2, half, span), BF),
-        vmem((parts, 2, half, span), F32),
-        vmem((parts, 2, half, span), F32),
-        pltpu.SemaphoreType.DMA((3 + parts,)),
+        vmem((parts, half, width), BF),
+        vmem((n_chunks, n_z, sub, span), BF),
+        vmem((n_chunks, n_z, sub, span), BF),
+        vmem((n_chunks, n_z, sub, span), BF),
+        vmem((n_chunks, n_z, sub, span), BF),
+        vmem((parts, span, half), F32),
+        vmem((parts, owner_span, half), F32),
+        pltpu.SemaphoreType.DMA((3 + n_chunks,)),
         pltpu.SemaphoreType.DMA((n_sem,)),
         pltpu.SemaphoreType.DMA((n_sem,)),
     ]
@@ -806,10 +836,10 @@
     anywhere = pl.BlockSpec(memory_space=pl.ANY)
     inside = pl.BlockSpec(memory_space=pltpu.VMEM)
     step_sum, control_sum, grad_rows = pl.pallas_call(
-        functools.partial(round_kernel, n_pos),
+        functools.partial(round_kernel, n_z),
         out_shape=(
-            jax.ShapeDtypeStruct((parts, half, owner_span), F32),
-            jax.ShapeDtypeStruct((parts, half, owner_span), F32),
+            jax.ShapeDtypeStruct((parts, owner_span, half), F32),
+            jax.ShapeDtypeStruct((parts, owner_span, half), F32),
             jax.ShapeDtypeStruct((parts, half, width), BF),
         ),
         in_specs=[smem, smem, anywhere, anywhere, inside, inside, inside, anywhere],
@@ -824,14 +854,15 @@
         emb_columns,
         target[0],
         norm_gain[None, :],
-        global_model,
-        global_control,
+        jnp.swapaxes(global_model, 1, 2),
+        jnp.swapaxes(global_control, 1, 2),
         client_control[0],
     )
-    slots = jnp.arange(n_clients)
-    own_steps = jnp.sum(jnp.where(slots == lax.axis_index("clients"), local_steps, 0))
-    update = grad_rows.astype(F32) / own_steps.astype(F32)
-    return (step_sum, control_sum, update[None])
+    return (
+        jnp.swapaxes(step_sum, 1, 2),
+        jnp.swapaxes(control_sum, 1, 2),
+        grad_rows.astype(F32)[None],
+    )
 
 
 def solution(mesh):
@@ -846,7 +877,7 @@
         P(),
         P(),
     )
-    paired = mesh.shape["fsdp"] == 2 and mesh.shape["clients"] % 2 == 0
+    paired = mesh.shape["fsdp"] == 2 and mesh.shape["clients"] % 4 == 0
     return jax.shard_map(
         paired_body if paired else general_body,
         mesh=mesh,

time: 223 us -> 175 us (0.78)
  the two profiles are of different devices: /device:TPU:29 before, /device:TPU:0 now
where the time goes in v1:
time: 175 us
  Pallas kernels  151 us (86%)
  local copies, waits for them, and re-layouts  13.3 us (8%)
  other arithmetic  5.17 us (3%)
  starting transfers between devices  4.9 us (3%)
    pallas_call x1, Pallas kernels, paired_body(): pl.pallas_call(functools.partial(round_kernel, n_z), out_shape=(jax.Shape...  151 us
    gather x1, local copies, waits for them, and re-layouts, paired_body(): emb_columns = embedding.at[ids].get(mode='promise_in_bounds')  10.6 us
    broadcast_in_dim x1, other arithmetic, paired_body(): grad_rows.astype(F32)[None]  4.44 us
    ppermute x1, starting transfers between devices, paired_body(): lax.ppermute(token_ids[0], ('clients', 'fsdp'), to_across)  4.24 us
  transfers between devices with their start and end apart: 2, of which 1 were waited for; matrix products, arithmetic and copies ran while one was open for 1% of the time, Pallas kernels for 0%

profile of v1, /device:TPU:0, one launch (start us, length us, event | category | flops | bytes accessed | tf_op | source)
XLA Modules:
  0.0 174.8 jit_solution(8116477465154855902)
XLA Ops:
  0.6 0.7 reduce
  1.3 0.7 collective-permute-start
  2.0 4.2 %collective-permute-start.1 = (s32[640]{0:T(1024)S(1)}, s32[640]{0:T(1024)S(1)}, u32[]{:S(2)}, u32[]{:S(2)}) collective-permute-start(s32[640]{0:T(1024)S(1)} %reduce), channel_id=1, source_target_pairs={{0,1},{1,3},{2,0},{3,2},{4,5},{5,7},{6,4},{7,6},{8,9},{9,11},{10,8... | collective-permute-start | bytes 7688 | tf_op jit(solution)/shard_map/ppermute | solution.py:795
  6.2 1.3 broadcast_in_dim.10.gain_ref
  7.5 0.0 collective-permute-done
  7.5 0.1 collective-permute-done.1
  7.6 10.6 %gather_fusion = bf16[1280,384]{1,0:T(8,128)(2,1)} fusion(bf16[16384,384]{1,0:T(8,128)(2,1)} %param.11, s32[2048]{0:T(1024)S(1)} %pad_clamp_fusion), kind=kCustom, calls=%fused_computation | custom fusion | bytes 1971200 | tf_op jit(solution)/shard_map/gather | solution.py:798
  18.2 150.7 %shard_map.112 = (f32[3,64,384]{2,1,0:T(8,128)}, f32[3,64,384]{2,1,0:T(8,128)}, bf16[3,384,1024]{2,1,0:T(8,128)(2,1)}) custom-call(s32[16]{0:T(128)} %steps_ref.1, s32[16]{0:T(128)} %weights_ref.1, bf16[1280,384]{1,0:T(8,128)(2,1)} %gather_fusion, bf16[640,768]{1,0:T(8,128)(2,1)} %bitcast.10, f32[1,768]{1,0:T(1,128)} %broadcast_in_dim.10.gain_ref, ...), custom_call_target="tpu_custom_call" | custom-call | tf_op jit(solution)/shard_map/pallas_call | solution.py:838
  168.9 0.0 copy-start.1
  168.9 0.0 copy-start
  168.9 4.4 %bitcast_convert_fusion = f32[1,3,384,1024]{3,2,1,0:T(8,128)} fusion(bf16[3,384,1024]{2,1,0:T(8,128)(2,1)} %get-tuple-element.8), kind=kLoop, calls=%fused_computation.1 | loop fusion | flops 1179648 | bytes 7077888 | tf_op jit(solution)/shard_map/broadcast_in_dim | solution.py:864
  173.4 0.0 copy-done.1
  173.4 0.7 copy.15
  174.1 0.0 copy-done
  174.1 0.7 copy.16
  (4 shorter events, 0.0 us)
Async XLA Ops:
  1.3 6.2 %collective-permute-start = (s32[640]{0:T(1024)S(1)}, s32[640]{0:T(1024)S(1)}, u32[]{:S(2)}, u32[]{:S(2)}) collective-permute-start(s32[640]{0:T(1024)S(1)} %reduce), channel_id=1, source_target_pairs={{0,0},{1,2},{2,1},{3,3},{4,4},{5,6},{6,5},{7,7},{8,8},{9,10},{10,9... | collective-permute-start | bytes 7688 | tf_op jit(solution)/shard_map/ppermute | solution.py:794
  2.0 5.6 %collective-permute-start.1 = (s32[640]{0:T(1024)S(1)}, s32[640]{0:T(1024)S(1)}, u32[]{:S(2)}, u32[]{:S(2)}) collective-permute-start(s32[640]{0:T(1024)S(1)} %reduce), channel_id=1, source_target_pairs={{0,1},{1,3},{2,0},{3,2},{4,5},{5,7},{6,4},{7,6},{8,9},{9,11},{10,8... | collective-permute-start | bytes 7688 | tf_op jit(solution)/shard_map/ppermute | solution.py:795
  168.9 4.5 %copy-start.1 = (f32[3,64,384]{2,1,0:T(8,128)S(1)}, f32[3,64,384]{2,1,0:T(8,128)}, u32[]{:S(2)}) copy-start(f32[3,64,384]{2,1,0:T(8,128)} %get-tuple-element.6) | copy-start | bytes 884740
  168.9 5.2 %copy-start = (f32[3,64,384]{2,1,0:T(8,128)S(1)}, f32[3,64,384]{2,1,0:T(8,128)}, u32[]{:S(2)}) copy-start(f32[3,64,384]{2,1,0:T(8,128)} %get-tuple-element.7) | copy-start | bytes 884740

commit v2 on v1

--- a/solution.py
+++ b/solution.py
@@ -230,6 +230,7 @@
     y_out,
     y_in,
     z_in,
+    summed,
     final,
     final_in,
     local_sem,
@@ -270,9 +271,8 @@
     def behind(d):
         return lax.rem(z + n_z - d, n_z)
 
-    def position(line, d):
-        row = y if line == 0 else 1 - y
-        return 2 * behind(d) + row
+    def position(line, row):
+        return 2 * row + (y if line == 0 else 1 - y)
 
     def columns(pos):
         return pl.ds(pl.multiple_of(pos * span, span), span)
@@ -311,40 +311,43 @@
     def target_copy():
         return remote(target_ref, target, "target", 0, swap)
 
+    quarter = half // 2
+    g_own = pl.ds(pl.multiple_of(jnp.where(home, 0, quarter), quarter), quarter)
+
     def g_window(pos):
-        return g_rows.at[:, :, columns(pos)]
+        return g_rows.at[:, g_own, columns(pos)]
 
     def model_window(group, pos):
         first, count = groups[group]
         return model.at[pl.ds(first, count), own_rows, columns(pos)]
 
-    def g_along(d, source):
-        window = g_window(source)
+    def g_along(d, row):
+        window = g_window(position(0, row))
         return remote(window, window, "gz", d, along(d))
 
-    def g_beside(d, source):
-        window = g_window(source)
-        return remote(window, window, "gy", d, beside)
-
-    def g_partner(line, d):
-        window = g_window(position(line, d))
-        return remote(window, window, "gp", line * n_z + d, partner)
+    def g_beside(line, row):
+        window = g_window(position(line, row))
+        return remote(window, window, "gy", row, beside)
+
+    def g_partner(line, row):
+        window = g_window(position(line, row))
+        return remote(window, window, "gp", line * n_z + row, partner)
 
     def cross_copy(group):
         window = model_window(group, p)
         return remote(window, window, "cross", group, across)
 
-    def model_along(group, d, source):
-        window = model_window(group, source)
+    def model_along(group, d, row):
+        window = model_window(group, position(0, row))
         return remote(window, window, "mz", group * n_z + d, along(d))
 
-    def model_beside(group, d, source):
-        window = model_window(group, source)
-        return remote(window, window, "my", group * n_z + d, beside)
-
-    def model_partner(group, line, d):
-        window = model_window(group, position(line, d))
-        return remote(window, window, "mp", group * n_pos + line * n_z + d, partner)
+    def model_beside(group, line, row):
+        window = model_window(group, position(line, row))
+        return remote(window, window, "my", group * n_z + row, beside)
+
+    def model_partner(group, line, row):
+        window = model_window(group, position(line, row))
+        return remote(window, window, "mp", group * n_pos + line * n_z + row, partner)
 
     def corr_copy(part):
         return remote(corr.at[part], role_corr.at[part], "corr", part, swap)
@@ -359,7 +362,7 @@
         return remote(window, window, "cur", part, partner)
 
     def sub_rows(s):
-        return pl.ds(s * sub, sub)
+        return pl.ds(pl.multiple_of(s * sub, sub), sub)
 
     def return_copy(part, s):
         return remote(
@@ -411,63 +414,61 @@
     packed[0, :, pl.ds(owner_at, owner_span), :] = model_ref[...].astype(BF)
     packed[1, :, pl.ds(owner_at, owner_span), :] = control_ref[...].astype(BF)
 
-    @pl.when(away)
-    def _():
-        pack_copy().start()
-        emb_copy().start()
-        target_copy().start()
-
+    pack_copy().start()
     own_load.start()
     emb_load.start()
+    pl.when(home)(target_load.start)
+    pack_copy().wait_recv()
 
     @pl.when(home)
     def _():
-        target_load.start()
-        partner_pack = packed.at[
-            :, :, pl.ds(pl.multiple_of((1 - b) * owner_span, owner_span), owner_span), :
-        ]
-        remote(partner_pack, partner_pack, "pack", 0, partner).wait_recv()
-        for part in range(parts):
-            g_rows[part, :, columns(p)] = packed[1, part].T
-        for d in range(1, n_z):
-            g_along(d, p).start()
-        g_beside(0, p).start()
         for part in range(parts):
             model[part, own_rows, columns(p)] = packed[0, part].T
         for group in range(2):
             cross_copy(group).start()
-        emb_copy().start()
-        for group in range(2):
-            for d in range(1, n_z):
-                model_along(group, d, p).start()
-        g_partner(0, 0).start()
-        for d in range(1, n_z):
-            g_along(d, position(0, d)).wait_recv()
-            g_beside(d, position(0, d)).start()
-            g_partner(0, d).start()
-        model_beside(0, 0, p).start()
-        model_beside(1, 0, p).start()
-        for d in range(n_z):
-            g_beside(d, position(1, d)).wait_recv()
-            g_partner(1, d).start()
+        for part in range(parts):
+            g_rows[part, :quarter, columns(p)] = packed[1, part].T[:quarter]
 
     @pl.when(away)
     def _():
-        for group in range(2):
-            cross_copy(group).wait_recv()
-            for d in range(1, n_z):
-                model_along(group, d, p).start()
-            model_beside(group, 0, p).start()
-
+        for part in range(parts):
+            g_rows[part, quarter:, columns(p)] = packed[1, part].T[quarter:]
+
+    for d in range(1, n_z):
+        g_along(d, z).start()
+    g_beside(0, z).start()
+    g_partner(0, z).start()
+    pl.when(home)(emb_copy().start)
     for group in range(2):
-        model_partner(group, 0, 0).start()
-    own_load.wait()
+        pl.when(away)(cross_copy(group).wait_recv)
+        for d in range(1, n_z):
+            model_along(group, d, z).start()
+        model_beside(group, 0, z).start()
+        model_partner(group, 0, z).start()
 
     @pl.when(away)
     def _():
+        emb_copy().start()
+        target_copy().start()
+
+    for d in range(1, n_z):
+        row = behind(d)
+        g_along(d, row).wait_recv()
+        g_beside(0, row).start()
+        g_partner(0, row).start()
+    for row in range(n_z):
+        g_beside(1, row).wait_recv()
+        g_partner(1, row).start()
+    for line in range(2):
+        for row in range(n_z):
+            g_partner(line, row).wait_recv()
+    for d in range(1, n_z):
+        g_along(d, z).wait_send()
+    for row in range(n_z):
+        g_beside(0, row).wait_send()
         for line in range(2):
-            for d in range(n_z):
-                g_partner(line, d).wait_recv()
+            g_partner(line, row).wait_send()
+    own_load.wait()
 
     chunk = half // 6
     for part in range(parts):
@@ -504,22 +505,27 @@
 
     lax.fori_loop(0, 5, normalise, 0)
 
-    def relay(group, d):
-        model_along(group, d, position(0, d)).wait_recv()
-        model_beside(group, d, position(0, d)).start()
-        model_partner(group, 0, d).start()
+    def relay(group):
+        for d in range(1, n_z):
+            row = behind(d)
+            model_along(group, d, row).wait_recv()
+            model_beside(group, 0, row).start()
+            model_partner(group, 0, row).start()
 
     def settle(group):
-        for d in range(n_z):
-            model_beside(group, d, position(1, d)).wait_recv()
-            model_partner(group, 1, d).start()
+        for row in range(n_z):
+            model_beside(group, 1, row).wait_recv()
+            model_partner(group, 1, row).start()
+
+    def arrive(group):
         for line in range(2):
-            for d in range(n_z):
-                model_partner(group, line, d).wait_recv()
-
-    for d in range(1, n_z):
-        relay(0, d)
+            for row in range(n_z):
+                model_partner(group, line, row).wait_recv()
+
+    relay(0)
     settle(0)
+    relay(1)
+    arrive(0)
 
     loss_scale = 1.0 / math.sqrt(2 * rows)
     n_tiles = width // TILE
@@ -534,7 +540,7 @@
 
         lax.fori_loop(0, n_tiles, product, 0)
 
-    def local_step(step, weights, finish):
+    def local_step(step, weights, finish, between):
         def forward(j, carry):
             cols = tile_at(j)
             gate_act, slope = gelu_parts(dot(normed[...], weights[0, :, cols]))
@@ -546,9 +552,8 @@
 
         lax.fori_loop(0, n_tiles, forward, 0)
         if step == 0:
-            for d in range(1, n_z):
-                relay(1, d)
             settle(1)
+            arrive(1)
 
             @pl.when(away)
             def _():
@@ -595,6 +600,7 @@
         lax.fori_loop(0, n_tiles, backward, 0)
         finish(2)
         term(0, normed_t, gate_grad)
+        between()
         term(1, normed_t, up_grad)
         finish(0)
         finish(1)
@@ -633,19 +639,22 @@
             def _():
                 return_copy(part, s).start()
 
-    local_step(0, model, update)
+    local_step(0, model, update, lambda: None)
     for part in range(parts):
         current_copy(part).wait_recv()
-    local_step(1, current, collect)
-
     weight = weights_ref[client].astype(F32)
     taken = steps_ref[client].astype(F32)
     inverse = 1.0 / taken
-    order = [(part, s) for part in (2, 0, 1) for s in range(n_sub)]
-
-    def share(part, s):
+
+    def place(k):
+        return lax.rem(k // n_sub + parts - 1, parts), lax.rem(k, n_sub)
+
+    def share(k):
+        part, s = place(k)
         at = sub_rows(s)
-        if s == 0:
+
+        @pl.when(s == 0)
+        def _():
             term_copy(1, part).wait_send()
 
         def spread(source):
@@ -671,12 +680,12 @@
         grad_store(part, s).start()
 
     def split(k):
-        part, s = order[k]
+        part, s = place(k)
         at = sub_rows(s)
         share_copy(part, s).wait_recv()
         for row in range(n_z):
             for line in range(2):
-                cols = columns(2 * row + (y if line == 0 else 1 - y))
+                cols = columns(position(line, row))
                 value = (
                     term_own[part, at, cols].astype(F32) + share_in[part, at, cols].astype(F32)
                 ).astype(BF)
@@ -693,21 +702,44 @@
             z_copy(k, d).start()
 
     def gather_z(k):
-        part, s = order[k]
+        part, s = place(k)
         value = kept[k, z].astype(F32)
         for d in range(1, n_z):
             z_copy(k, d).wait_recv()
             value += z_in[k, d].astype(F32)
-        final[part, :, sub_rows(s)] = value.T
-
-    for k in range(n_chunks + 2):
-        if k < n_chunks:
-            share(*order[k])
-            split(k)
-        if 0 <= k - 1 < n_chunks:
-            spread_z(k - 1)
-        if 0 <= k - 2:
-            gather_z(k - 2)
+        summed[part, sub_rows(s), :] = value
+
+    split_lag, y_lag, z_lag = 1, 3, 6
+
+    def advance(k):
+        @pl.when(k < n_chunks)
+        def _():
+            share(k)
+
+        @pl.when((k >= split_lag) & (k - split_lag < n_chunks))
+        def _():
+            split(k - split_lag)
+
+        @pl.when((k >= y_lag) & (k - y_lag < n_chunks))
+        def _():
+            spread_z(k - y_lag)
+
+        @pl.when(k >= z_lag)
+        def _():
+            gather_z(k - z_lag)
+
+    def early():
+        share(0)
+
+    local_step(1, current, collect, early)
+
+    def loop(k, carry):
+        advance(k)
+        return carry
+
+    lax.fori_loop(1, n_chunks + z_lag, loop, 0)
+    for part in range(parts):
+        final[part] = summed[part].T
     final_copy().start()
 
     weight_total = weights_ref[0]
@@ -727,7 +759,6 @@
 
     @pl.when(away)
     def _():
-        pack_copy().wait_send()
         target_copy().wait_send()
         for part in range(parts):
             corr_copy(part).wait_send()
@@ -738,21 +769,16 @@
     def _():
         for group in range(2):
             cross_copy(group).wait_send()
-        for d in range(n_z):
-            if d > 0:
-                g_along(d, p).wait_send()
-            g_beside(d, position(0, d)).wait_send()
-            for line in range(2):
-                g_partner(line, d).wait_send()
-
+
+    pack_copy().wait_send()
     emb_copy().wait_send()
     for group in range(2):
-        for d in range(n_z):
-            if d > 0:
-                model_along(group, d, p).wait_send()
-            model_beside(group, d, position(0, d)).wait_send()
+        for d in range(1, n_z):
+            model_along(group, d, z).wait_send()
+        for row in range(n_z):
+            model_beside(group, 0, row).wait_send()
             for line in range(2):
-                model_partner(group, line, d).wait_send()
+                model_partner(group, line, row).wait_send()
     for part in range(parts):
         current_copy(part).wait_send()
         for s in range(n_sub):
@@ -784,7 +810,7 @@
     span = 2 * owner_span
     rows = token_ids.shape[1]
     depth = 2 * half
-    sub = 128
+    sub = 64
     n_chunks = parts * (half // sub)
     pairs = [(c, f) for c in range(n_clients) for f in range(2)]
     to_role = [(c * 2 + f, (c - c % 2 + f) * 2 + c % 2) for c, f in pairs]
@@ -826,6 +852,7 @@
         vmem((n_chunks, n_z, sub, span), BF),
         vmem((n_chunks, n_z, sub, span), BF),
         vmem((n_chunks, n_z, sub, span), BF),
+        vmem((parts, half, span), F32),
         vmem((parts, span, half), F32),
         vmem((parts, owner_span, half), F32),
         pltpu.SemaphoreType.DMA((3 + n_chunks,)),

time: 175 us -> 158 us (0.903)
  Pallas kernels: 151 us -> 133 us
    pallas_call x1, Pallas kernels: 151 us -> 133 us  [paired_body(): pl.pallas_call(functools.partial(round_kernel, n_z), out_shape=(jax.Shape...]
where the time goes in v2:
time: 158 us; the launch traced here: 157 us
  Pallas kernels  133 us (84%)
  local copies, waits for them, and re-layouts  13.3 us (8%)
  other arithmetic  5.17 us (3%)
  starting transfers between devices  4.9 us (3%)
    pallas_call x1, Pallas kernels, paired_body(): pl.pallas_call(functools.partial(round_kernel, n_z), out_shape=(jax.Shape...  133 us
    gather x1, local copies, waits for them, and re-layouts, paired_body(): emb_columns = embedding.at[ids].get(mode='promise_in_bounds')  10.6 us
    broadcast_in_dim x1, other arithmetic, paired_body(): grad_rows.astype(F32)[None]  4.44 us
    ppermute x1, starting transfers between devices, paired_body(): lax.ppermute(token_ids[0], ('clients', 'fsdp'), to_across)  4.24 us
  transfers between devices with their start and end apart: 2, of which 1 were waited for; matrix products, arithmetic and copies ran while one was open for 1% of the time, Pallas kernels for 0%

profile of v2, /device:TPU:0, one launch (start us, length us, event | category | flops | bytes accessed | tf_op | source)
XLA Modules:
  0.0 157.4 jit_solution(12437195003729002122)
XLA Ops:
  0.6 0.7 reduce
  1.3 0.7 collective-permute-start
  2.0 4.2 %collective-permute-start.1 = (s32[640]{0:T(1024)S(1)}, s32[640]{0:T(1024)S(1)}, u32[]{:S(2)}, u32[]{:S(2)}) collective-permute-start(s32[640]{0:T(1024)S(1)} %reduce), channel_id=1, source_target_pairs={{0,1},{1,3},{2,0},{3,2},{4,5},{5,7},{6,4},{7,6},{8,9},{9,11},{10,8... | collective-permute-start | bytes 7688 | tf_op jit(solution)/shard_map/ppermute | solution.py:821
  6.2 1.3 broadcast_in_dim.10.gain_ref
  7.5 0.0 collective-permute-done
  7.5 0.1 collective-permute-done.1
  7.6 10.6 %gather_fusion = bf16[1280,384]{1,0:T(8,128)(2,1)} fusion(bf16[16384,384]{1,0:T(8,128)(2,1)} %param.11, s32[2048]{0:T(1024)S(1)} %pad_clamp_fusion), kind=kCustom, calls=%fused_computation | custom fusion | bytes 1971200 | tf_op jit(solution)/shard_map/gather | solution.py:824
  18.2 133.3 %shard_map.112 = (f32[3,64,384]{2,1,0:T(8,128)}, f32[3,64,384]{2,1,0:T(8,128)}, bf16[3,384,1024]{2,1,0:T(8,128)(2,1)}) custom-call(s32[16]{0:T(128)} %steps_ref.1, s32[16]{0:T(128)} %weights_ref.1, bf16[1280,384]{1,0:T(8,128)(2,1)} %gather_fusion, bf16[640,768]{1,0:T(8,128)(2,1)} %bitcast.10, f32[1,768]{1,0:T(1,128)} %broadcast_in_dim.10.gain_ref, ...), custom_call_target="tpu_custom_call" | custom-call | tf_op jit(solution)/shard_map/pallas_call | solution.py:865
  151.5 0.0 copy-start.1
  151.5 0.0 copy-start
  151.5 4.4 %bitcast_convert_fusion = f32[1,3,384,1024]{3,2,1,0:T(8,128)} fusion(bf16[3,384,1024]{2,1,0:T(8,128)(2,1)} %get-tuple-element.8), kind=kLoop, calls=%fused_computation.1 | loop fusion | flops 1179648 | bytes 7077888 | tf_op jit(solution)/shard_map/broadcast_in_dim | solution.py:891
  155.9 0.0 copy-done.1
  156.0 0.7 copy.15
  156.7 0.0 copy-done
  156.7 0.7 copy.16
  (4 shorter events, 0.0 us)
Async XLA Ops:
  1.3 6.2 %collective-permute-start = (s32[640]{0:T(1024)S(1)}, s32[640]{0:T(1024)S(1)}, u32[]{:S(2)}, u32[]{:S(2)}) collective-permute-start(s32[640]{0:T(1024)S(1)} %reduce), channel_id=1, source_target_pairs={{0,0},{1,2},{2,1},{3,3},{4,4},{5,6},{6,5},{7,7},{8,8},{9,10},{10,9... | collective-permute-start | bytes 7688 | tf_op jit(solution)/shard_map/ppermute | solution.py:820
  2.0 5.6 %collective-permute-start.1 = (s32[640]{0:T(1024)S(1)}, s32[640]{0:T(1024)S(1)}, u32[]{:S(2)}, u32[]{:S(2)}) collective-permute-start(s32[640]{0:T(1024)S(1)} %reduce), channel_id=1, source_target_pairs={{0,1},{1,3},{2,0},{3,2},{4,5},{5,7},{6,4},{7,6},{8,9},{9,11},{10,8... | collective-permute-start | bytes 7688 | tf_op jit(solution)/shard_map/ppermute | solution.py:821
  151.5 4.5 %copy-start.1 = (f32[3,64,384]{2,1,0:T(8,128)S(1)}, f32[3,64,384]{2,1,0:T(8,128)}, u32[]{:S(2)}) copy-start(f32[3,64,384]{2,1,0:T(8,128)} %get-tuple-element.6) | copy-start | bytes 884740
  151.5 5.2 %copy-start = (f32[3,64,384]{2,1,0:T(8,128)S(1)}, f32[3,64,384]{2,1,0:T(8,128)}, u32[]{:S(2)}) copy-start(f32[3,64,384]{2,1,0:T(8,128)} %get-tuple-element.7) | copy-start | bytes 884740

commit v3 on v2

--- a/solution.py
+++ b/solution.py
@@ -225,7 +225,6 @@
     term_out,
     term_own,
     term_in,
-    share_in,
     kept,
     y_out,
     y_in,
@@ -282,7 +281,7 @@
     counts = dict(
         pack=1, emb=1, target=1, cross=2, gz=n_z, gy=n_z, gp=n_pos, mz=2 * n_z, my=2 * n_z,
         mp=2 * n_pos, corr=parts, term0=parts, term1=parts, cur=parts, ret=n_chunks,
-        share=n_chunks, ry=n_chunks, rz=n_chunks * n_z, final=1,
+        share=n_chunks, ry=n_chunks, rz=n_chunks * n_z, final=parts,
     )
     base = {}
     total = 0
@@ -354,7 +353,7 @@
 
     def term_copy(step, part):
         return remote(
-            term_out.at[part], term_in.at[step, part], "term%d" % step, part, partner
+            term_out.at[part], term_in.at[part], "term%d" % step, part, partner
         )
 
     def current_copy(part):
@@ -372,7 +371,7 @@
 
     def share_copy(part, s):
         return remote(
-            term_out.at[part, sub_rows(s), :], share_in.at[part, sub_rows(s), :],
+            term_out.at[part, sub_rows(s), :], model.at[part, sub_rows(s), :],
             "share", part * n_sub + s, partner,
         )
 
@@ -384,15 +383,13 @@
             kept.at[k, lax.rem(z + d, n_z)], z_in.at[k, d], "rz", k * n_z + d, along(d)
         )
 
-    def final_copy():
-        return remote(
-            final.at[:, pl.ds(pl.multiple_of((1 - b) * owner_span, owner_span), owner_span), :],
-            final_in, "final", 0, partner,
-        )
+    def final_copy(part):
+        at = pl.ds(pl.multiple_of((1 - b) * owner_span, owner_span), owner_span)
+        return remote(final.at[part, at, :], final_in.at[part], "final", part, partner)
 
     def grad_store(part, s):
         return pltpu.make_async_copy(
-            term_in.at[0, part, sub_rows(s), :], grad_out.at[part, sub_rows(s), :],
+            term_in.at[part, sub_rows(s), :], grad_out.at[part, sub_rows(s), :],
             local_sem.at[3 + part * n_sub + s],
         )
 
@@ -471,7 +468,7 @@
     own_load.wait()
 
     chunk = half // 6
-    for part in range(parts):
+    for part in (2, 0, 1):
 
         def correct(i, carry):
             at = pl.ds(pl.multiple_of(i * chunk, chunk), chunk)
@@ -498,7 +495,7 @@
         at = pl.ds(pl.multiple_of(i * block, block), block)
         widened = emb[at, :].astype(F32)
         inv_norm = lax.rsqrt(jnp.mean(widened * widened, axis=1, keepdims=True) + norm_eps)
-        value = (widened * inv_norm * gain_ref[...]).astype(BF)
+        value = (widened * inv_norm * gain_ref[...][None, :]).astype(BF)
         normed[at, :] = value
         normed_t[:, at] = value.T
         return carry
@@ -538,19 +535,19 @@
             store(j, dot(left[left_rows, :], right[:, tile_at(j)]).astype(BF))
             return carry
 
-        lax.fori_loop(0, n_tiles, product, 0)
+        lax.fori_loop(0, n_tiles, product, 0, unroll=True)
 
     def local_step(step, weights, finish, between):
         def forward(j, carry):
             cols = tile_at(j)
             gate_act, slope = gelu_parts(dot(normed[...], weights[0, :, cols]))
             up_pre = dot(normed[...], weights[1, :, cols])
-            act[:, cols] = gate_act
-            slope_up[:, cols] = slope * up_pre
+            act[:, cols] = gate_act.astype(BF)
+            slope_up[:, cols] = (slope * up_pre).astype(BF)
             hidden[:, cols] = (gate_act * up_pre).astype(BF)
             return carry
 
-        lax.fori_loop(0, n_tiles, forward, 0)
+        lax.fori_loop(0, n_tiles, forward, 0, unroll=True)
         if step == 0:
             settle(1)
             arrive(1)
@@ -573,22 +570,27 @@
             out_grad_t[cols, :] = value.T
             return carry
 
-        lax.fori_loop(0, depth // TILE, project, 0)
-
-        def term(part, left, right):
-            def store_out(j, value):
+        lax.fori_loop(0, depth // TILE, project, 0, unroll=True)
+
+        def term_other(part, left, right):
+            def store(j, value):
                 term_out[part, :, tile_at(j)] = value
-
-            def store_own(j, value):
-                term_own[part, :, tile_at(j)] = value
 
             if step > 0:
                 term_copy(step - 1, part).wait_send()
-            half_product(left, other_rows, right, store_out)
+            half_product(left, other_rows, right, store)
             term_copy(step, part).start()
-            half_product(left, own_rows, right, store_own)
-
-        term(2, out_grad_t, hidden)
+
+        def term_mine(part, left, right):
+            def store(j, value):
+                term_own[part, :, tile_at(j)] = value
+
+            half_product(left, own_rows, right, store)
+
+        term_other(2, out_grad_t, hidden)
+        term_mine(2, out_grad_t, hidden)
+        if step > 0:
+            finish(2)
 
         def backward(j, carry):
             cols = tile_at(j)
@@ -597,11 +599,16 @@
             up_grad[:, cols] = (hidden_grad * act[:, cols]).astype(BF)
             return carry
 
-        lax.fori_loop(0, n_tiles, backward, 0)
-        finish(2)
-        term(0, normed_t, gate_grad)
-        between()
-        term(1, normed_t, up_grad)
+        lax.fori_loop(0, n_tiles, backward, 0, unroll=True)
+        if step == 0:
+            finish(2)
+        term_other(0, normed_t, gate_grad)
+        term_other(1, normed_t, up_grad)
+        between(0)
+        term_mine(0, normed_t, gate_grad)
+        between(1)
+        term_mine(1, normed_t, up_grad)
+        between(2)
         finish(0)
         finish(1)
 
@@ -615,7 +622,7 @@
         def apply(i, carry):
             at = pl.ds(pl.multiple_of(i * chunk, chunk), chunk)
             model_at = pl.ds(pl.multiple_of(half_at + i * chunk, chunk), chunk)
-            grads = term_own[part, at, :].astype(F32) + term_in[0, part, at, :].astype(F32)
+            grads = term_own[part, at, :].astype(F32) + term_in[part, at, :].astype(F32)
             c_rows[part, at, :] = grads
             pseudo = grads + role_corr[part, at, :].astype(F32)
             current[part, model_at, :] = (
@@ -632,14 +639,31 @@
         term_copy(1, part).wait_recv()
         for s in range(n_sub):
             at = sub_rows(s)
-            grads = term_own[part, at, :].astype(F32) + term_in[1, part, at, :].astype(F32)
+            grads = term_own[part, at, :].astype(F32) + term_in[part, at, :].astype(F32)
             role_corr[part, at, :] = (c_rows[part, at, :] + second * grads).astype(BF)
 
             @pl.when(away)
             def _():
                 return_copy(part, s).start()
 
-    local_step(0, model, update, lambda: None)
+    local_step(0, model, update, lambda k: None)
+    pack_copy().wait_send()
+    emb_copy().wait_send()
+    for group in range(2):
+        pl.when(home)(cross_copy(group).wait_send)
+        for d in range(1, n_z):
+            model_along(group, d, z).wait_send()
+        for row in range(n_z):
+            model_beside(group, 0, row).wait_send()
+            for line in range(2):
+                model_partner(group, line, row).wait_send()
+
+    @pl.when(away)
+    def _():
+        target_copy().wait_send()
+        for part in range(parts):
+            corr_copy(part).wait_send()
+
     for part in range(parts):
         current_copy(part).wait_recv()
     weight = weights_ref[client].astype(F32)
@@ -661,7 +685,7 @@
             value = source[part, at, :].astype(F32)
             averaged = inverse * value
             summed = value + taken * corr[part, at, :].astype(F32)
-            term_in[0, part, at, :] = averaged.astype(BF)
+            term_in[part, at, :] = averaged.astype(BF)
             mine = jnp.where(b == 0, summed, averaged)
             theirs = jnp.where(b == 0, averaged, summed)
             term_own[part, at, :] = (weight * mine).astype(BF)
@@ -687,7 +711,7 @@
             for line in range(2):
                 cols = columns(position(line, row))
                 value = (
-                    term_own[part, at, cols].astype(F32) + share_in[part, at, cols].astype(F32)
+                    term_own[part, at, cols].astype(F32) + model[part, at, cols].astype(F32)
                 ).astype(BF)
                 if line == 0:
                     kept[k, row] = value
@@ -708,6 +732,17 @@
             z_copy(k, d).wait_recv()
             value += z_in[k, d].astype(F32)
         summed[part, sub_rows(s), :] = value
+        y_copy(k).wait_send()
+        for d in range(1, n_z):
+            z_copy(k, d).wait_send()
+        share_copy(part, s).wait_send()
+        grad_store(part, s).wait()
+        pl.when(away)(return_copy(part, s).wait_send)
+
+        @pl.when(s == n_sub - 1)
+        def _():
+            final[part] = summed[part].T
+            final_copy(part).start()
 
     split_lag, y_lag, z_lag = 1, 3, 6
 
@@ -728,19 +763,15 @@
         def _():
             gather_z(k - z_lag)
 
-    def early():
-        share(0)
-
-    local_step(1, current, collect, early)
+    local_step(1, current, collect, advance)
+    for part in range(parts):
+        current_copy(part).wait_send()
 
     def loop(k, carry):
         advance(k)
         return carry
 
-    lax.fori_loop(1, n_chunks + z_lag, loop, 0)
-    for part in range(parts):
-        final[part] = summed[part].T
-    final_copy().start()
+    lax.fori_loop(3, n_chunks + z_lag, loop, 0)
 
     weight_total = weights_ref[0]
     step_total = weights_ref[0] * steps_ref[0]
@@ -751,44 +782,24 @@
     step_total = step_total.astype(F32)
     control = control_ref[...]
     lost = step_total * (control - control.astype(BF).astype(F32))
-    final_copy().wait_recv()
+    for part in range(parts):
+        final_copy(part).wait_recv()
     mine = final[:, pl.ds(owner_at, owner_span), :]
     theirs = final_in[...]
     step_out[...] = (jnp.where(b == 0, mine, theirs) + lost) / weight_total
     control_out[...] = jnp.where(b == 0, theirs, mine) / weight_total
 
-    @pl.when(away)
+    for part in range(parts):
+        final_copy(part).wait_send()
+
+
+def widen_kernel(step_ref, control_ref, grad_ref, step_out, control_out, grad_out):
+    @pl.when(pl.program_id(0) == 0)
     def _():
-        target_copy().wait_send()
-        for part in range(parts):
-            corr_copy(part).wait_send()
-            for s in range(n_sub):
-                return_copy(part, s).wait_send()
-
-    @pl.when(home)
-    def _():
-        for group in range(2):
-            cross_copy(group).wait_send()
-
-    pack_copy().wait_send()
-    emb_copy().wait_send()
-    for group in range(2):
-        for d in range(1, n_z):
-            model_along(group, d, z).wait_send()
-        for row in range(n_z):
-            model_beside(group, 0, row).wait_send()
-            for line in range(2):
-                model_partner(group, line, row).wait_send()
-    for part in range(parts):
-        current_copy(part).wait_send()
-        for s in range(n_sub):
-            share_copy(part, s).wait_send()
-            grad_store(part, s).wait()
-    for k in range(n_chunks):
-        y_copy(k).wait_send()
-        for d in range(1, n_z):
-            z_copy(k, d).wait_send()
-    final_copy().wait_send()
+        step_out[...] = step_ref[...]
+        control_out[...] = control_ref[...]
+
+    grad_out[...] = grad_ref[...].astype(F32)
 
 
 def paired_body(
@@ -823,7 +834,7 @@
     )
     emb_columns = embedding.at[ids].get(mode="promise_in_bounds")
 
-    n_sem = 6 + 6 * n_z + 3 * n_pos + 4 * parts + n_chunks * (3 + n_z)
+    n_sem = 5 + 6 * n_z + 3 * n_pos + 5 * parts + n_chunks * (3 + n_z)
     vmem = pltpu.VMEM
     scratch = [
         vmem((2, parts, span, half), BF),
@@ -837,8 +848,8 @@
         vmem((rows, depth), BF),
         vmem((rows, depth), BF),
         vmem((depth, rows), BF),
-        vmem((rows, width), F32),
-        vmem((rows, width), F32),
+        vmem((rows, width), BF),
+        vmem((rows, width), BF),
         vmem((rows, width), BF),
         vmem((rows, depth), BF),
         vmem((depth, rows), BF),
@@ -846,7 +857,6 @@
         vmem((rows, width), BF),
         vmem((parts, half, width), BF),
         vmem((parts, half, width), BF),
-        vmem((2, parts, half, width), BF),
         vmem((parts, half, width), BF),
         vmem((n_chunks, n_z, sub, span), BF),
         vmem((n_chunks, n_z, sub, span), BF),
@@ -880,15 +890,29 @@
         client_weight,
         emb_columns,
         target[0],
-        norm_gain[None, :],
+        norm_gain,
         jnp.swapaxes(global_model, 1, 2),
         jnp.swapaxes(global_control, 1, 2),
         client_control[0],
     )
+    block = half // 2
+    small = pl.BlockSpec((parts, owner_span, half), lambda i: (0, 0, 0))
+    large = pl.BlockSpec((block, width), lambda i: (i, 0))
+    step_sum, control_sum, update = pl.pallas_call(
+        widen_kernel,
+        out_shape=(
+            jax.ShapeDtypeStruct((parts, owner_span, half), F32),
+            jax.ShapeDtypeStruct((parts, owner_span, half), F32),
+            jax.ShapeDtypeStruct((parts * half, width), F32),
+        ),
+        grid=(parts * half // block,),
+        in_specs=[small, small, large],
+        out_specs=(small, small, large),
+    )(step_sum, control_sum, grad_rows.reshape(parts * half, width))
     return (
         jnp.swapaxes(step_sum, 1, 2),
         jnp.swapaxes(control_sum, 1, 2),
-        grad_rows.astype(F32)[None],
+        update.reshape(1, parts, half, width),
     )
 
 

time: 158 us -> 148 us (0.937)
  other arithmetic: 5.17 us -> 0.73 us
  Pallas kernels: 133 us -> 130 us
  local copies, waits for them, and re-layouts: 13.3 us -> 10.6 us
    pallas_call x1, Pallas kernels: 133 us -> 124 us  [paired_body(): pl.pallas_call(functools.partial(round_kernel, n_z), out_shape=(jax.Shape...]
    pallas_call x0 -> x1, Pallas kernels: none -> 5.67 us  [paired_body(): pl.pallas_call(widen_kernel, out_shape=(jax.ShapeDtypeStruct((parts, owne...]
    broadcast_in_dim x1 -> x0, other arithmetic: 4.44 us -> none  [paired_body(): grad_rows.astype(F32)[None]]
  transfers between devices with their start and end apart: 2 -> 2, of which waited for: 1 -> 1; matrix products, arithmetic and copies ran while one was open for 1% -> 0% of each run, Pallas kernels for 0% -> 0%
where the time goes in v3:
time: 148 us
  Pallas kernels  130 us (88%)
  local copies, waits for them, and re-layouts  10.6 us (7%)
  starting transfers between devices  4.9 us (3%)
    pallas_call x1, Pallas kernels, paired_body(): pl.pallas_call(functools.partial(round_kernel, n_z), out_shape=(jax.Shape...  124 us
    gather x1, local copies, waits for them, and re-layouts, paired_body(): emb_columns = embedding.at[ids].get(mode='promise_in_bounds')  10.6 us
    pallas_call x1, Pallas kernels, paired_body(): pl.pallas_call(widen_kernel, out_shape=(jax.ShapeDtypeStruct((parts, owne...  5.67 us
    ppermute x1, starting transfers between devices, paired_body(): lax.ppermute(token_ids[0], ('clients', 'fsdp'), to_across)  4.24 us
  transfers between devices with their start and end apart: 2, of which 1 were waited for; matrix products, arithmetic and copies ran while one was open for 0% of the time, Pallas kernels for 0%

profile of v3, /device:TPU:0, one launch (start us, length us, event | category | flops | bytes accessed | tf_op | source)
XLA Modules:
  0.0 147.8 jit_solution(17099306948963363843)
XLA Ops:
  0.6 0.7 reduce
  1.3 0.7 collective-permute-start
  2.0 4.2 %collective-permute-start.1 = (s32[640]{0:T(1024)S(1)}, s32[640]{0:T(1024)S(1)}, u32[]{:S(2)}, u32[]{:S(2)}) collective-permute-start(s32[640]{0:T(1024)S(1)} %reduce), channel_id=1, source_target_pairs={{0,1},{1,3},{2,0},{3,2},{4,5},{5,7},{6,4},{7,6},{8,9},{9,11},{10,8... | collective-permute-start | bytes 7688 | tf_op jit(solution)/shard_map/ppermute | solution.py:832
  6.2 0.0 collective-permute-done
  6.2 1.3 collective-permute-done.1
  7.6 10.6 %gather_fusion = bf16[1280,384]{1,0:T(8,128)(2,1)} fusion(bf16[16384,384]{1,0:T(8,128)(2,1)} %param.11, s32[2048]{0:T(1024)S(1)} %pad_clamp_fusion), kind=kCustom, calls=%fused_computation | custom fusion | bytes 1971200 | tf_op jit(solution)/shard_map/gather | solution.py:835
  18.2 123.9 %shard_map.112 = (f32[3,64,384]{2,1,0:T(8,128)}, f32[3,64,384]{2,1,0:T(8,128)}, bf16[3,384,1024]{2,1,0:T(8,128)(2,1)}) custom-call(s32[16]{0:T(128)} %steps_ref.1, s32[16]{0:T(128)} %weights_ref.1, bf16[1280,384]{1,0:T(8,128)(2,1)} %gather_fusion, bf16[640,768]{1,0:T(8,128)(2,1)} %bitcast.10, f32[768]{0:T(1024)} %gain_ref.1, f32[3,64,384]{2,1,0:T(8,128)} %bitcast.11, ...), custom_call_target="tpu_custom_call" | custom-call | tf_op jit(solution)/shard_map/pallas_call | solution.py:875
  142.1 5.7 %shard_map.113 = (f32[3,64,384]{2,1,0:T(8,128)}, f32[3,64,384]{2,1,0:T(8,128)}, f32[1152,1024]{1,0:T(8,128)}) custom-call(f32[3,64,384]{2,1,0:T(8,128)} %get-tuple-element.9.step_ref, f32[3,64,384]{2,1,0:T(8,128)} %get-tuple-element.10.control_ref, bf16[1152,1024]{1,0:T(8,128)(2,1)} %bitcast.9), custom_call_target="tpu_custom_call" | custom-call | tf_op jit(solution)/shard_map/pallas_call | solution.py:901
  (4 shorter events, 0.0 us)
Async XLA Ops:
  1.3 4.9 %collective-permute-start = (s32[640]{0:T(1024)S(1)}, s32[640]{0:T(1024)S(1)}, u32[]{:S(2)}, u32[]{:S(2)}) collective-permute-start(s32[640]{0:T(1024)S(1)} %reduce), channel_id=1, source_target_pairs={{0,0},{1,2},{2,1},{3,3},{4,4},{5,6},{6,5},{7,7},{8,8},{9,10},{10,9... | collective-permute-start | bytes 7688 | tf_op jit(solution)/shard_map/ppermute | solution.py:831
  2.0 5.6 %collective-permute-start.1 = (s32[640]{0:T(1024)S(1)}, s32[640]{0:T(1024)S(1)}, u32[]{:S(2)}, u32[]{:S(2)}) collective-permute-start(s32[640]{0:T(1024)S(1)} %reduce), channel_id=1, source_target_pairs={{0,1},{1,3},{2,0},{3,2},{4,5},{5,7},{6,4},{7,6},{8,9},{9,11},{10,8... | collective-permute-start | bytes 7688 | tf_op jit(solution)/shard_map/ppermute | solution.py:832

commit v4 on v3

--- a/solution.py
+++ b/solution.py
@@ -191,11 +191,21 @@
     )
 
 
+def semaphore_counts(parts, n_z, n_chunks):
+    arrivals = dict(
+        ids=2, pack=1, emb=1, target=1, cross=2, gz=n_z, gy=n_z, gp=1, mz=2 * n_z, my=2 * n_z,
+        mp=2, corr=parts, term0=parts, term1=parts, cur=1, ret=n_chunks, share=n_chunks,
+        ry=n_chunks, rz=n_chunks, final=1,
+    )
+    return arrivals, len(arrivals) + 2 * parts + 2
+
+
 def round_kernel(
     n_z,
     steps_ref,
     weights_ref,
-    emb_ref,
+    ids_ref,
+    table_ref,
     target_ref,
     gain_ref,
     model_ref,
@@ -204,6 +214,10 @@
     step_out,
     control_out,
     grad_out,
+    table,
+    ids_in,
+    ids,
+    emb_out,
     packed,
     model,
     current,
@@ -278,33 +292,40 @@
 
     n_chunks = parts * n_sub
     groups = ((0, parts - 1), (parts - 1, 1))
-    counts = dict(
-        pack=1, emb=1, target=1, cross=2, gz=n_z, gy=n_z, gp=n_pos, mz=2 * n_z, my=2 * n_z,
-        mp=2 * n_pos, corr=parts, term0=parts, term1=parts, cur=parts, ret=n_chunks,
-        share=n_chunks, ry=n_chunks, rz=n_chunks * n_z, final=parts,
-    )
+    arrivals, _ = semaphore_counts(parts, n_z, n_chunks)
     base = {}
     total = 0
-    for name, count in counts.items():
+    for name, count in arrivals.items():
         base[name] = total
         total += count
-
-    def remote(src, dst, name, index, device):
-        k = base[name] + index
+    kinds = list(arrivals)
+
+    def remote(src, dst, name, index, device, leave=None):
+        if leave is None:
+            leave = kinds.index(name)
         return pltpu.make_async_remote_copy(
-            src_ref=src, dst_ref=dst, send_sem=send_sem.at[k], recv_sem=recv_sem.at[k],
+            src_ref=src, dst_ref=dst, send_sem=send_sem.at[leave],
+            recv_sem=recv_sem.at[base[name] + index],
             device_id=device, device_id_type=MESH,
         )
+
+    def all_sent(window, name):
+        remote(window, window, name, 0, partner).wait_send()
 
     def pack_copy():
         window = packed.at[:, :, pl.ds(owner_at, owner_span), :]
         return remote(window, window, "pack", 0, partner)
 
+    emb_columns = pl.ds(pl.multiple_of(x * half, half), half)
+
+    def ids_copy(slot, device):
+        return remote(
+            ids_ref, ids_in.at[slot], "ids", slot, device, len(kinds) + 2 * parts + slot
+        )
+
     def emb_copy():
         return remote(
-            emb_ref.at[pl.ds(rows, rows), :],
-            emb.at[:, pl.ds(pl.multiple_of(x * half, half), half)],
-            "emb", 0, across,
+            emb_out, emb.at[:, emb_columns], "emb", 0, across,
         )
 
     def target_copy():
@@ -330,7 +351,7 @@
 
     def g_partner(line, row):
         window = g_window(position(line, row))
-        return remote(window, window, "gp", line * n_z + row, partner)
+        return remote(window, window, "gp", 0, partner)
 
     def cross_copy(group):
         window = model_window(group, p)
@@ -346,19 +367,20 @@
 
     def model_partner(group, line, row):
         window = model_window(group, position(line, row))
-        return remote(window, window, "mp", group * n_pos + line * n_z + row, partner)
+        return remote(window, window, "mp", group, partner)
 
     def corr_copy(part):
         return remote(corr.at[part], role_corr.at[part], "corr", part, swap)
 
     def term_copy(step, part):
         return remote(
-            term_out.at[part], term_in.at[part], "term%d" % step, part, partner
+            term_out.at[part], term_in.at[part], "term%d" % step, part, partner,
+            len(kinds) + step * parts + part,
         )
 
     def current_copy(part):
         window = current.at[part, own_rows, :]
-        return remote(window, window, "cur", part, partner)
+        return remote(window, window, "cur", 0, partner)
 
     def sub_rows(s):
         return pl.ds(pl.multiple_of(s * sub, sub), sub)
@@ -380,17 +402,17 @@
 
     def z_copy(k, d):
         return remote(
-            kept.at[k, lax.rem(z + d, n_z)], z_in.at[k, d], "rz", k * n_z + d, along(d)
+            kept.at[k, lax.rem(z + d, n_z)], z_in.at[k, d], "rz", k, along(d)
         )
 
     def final_copy(part):
         at = pl.ds(pl.multiple_of((1 - b) * owner_span, owner_span), owner_span)
-        return remote(final.at[part, at, :], final_in.at[part], "final", part, partner)
+        return remote(final.at[part, at, :], final_in.at[part], "final", 0, partner)
 
     def grad_store(part, s):
         return pltpu.make_async_copy(
             term_in.at[part, sub_rows(s), :], grad_out.at[part, sub_rows(s), :],
-            local_sem.at[3 + part * n_sub + s],
+            local_sem.at[4],
         )
 
     barrier = pltpu.get_barrier_semaphore()
@@ -401,11 +423,19 @@
     pl.semaphore_wait(barrier, 3 + n_z)
 
     own_load = pltpu.make_async_copy(own_ref, c_rows, local_sem.at[0])
-    emb_load = pltpu.make_async_copy(
-        emb_ref.at[pl.ds(0, rows), :],
-        emb.at[:, pl.ds(pl.multiple_of(x * half, half), half)],
-        local_sem.at[1],
-    )
+    table_load = pltpu.make_async_copy(table_ref, table, local_sem.at[1])
+    table_load.start()
+
+    @pl.when(home)
+    def _():
+        ids_copy(1, across).start()
+        ids_in[0] = ids_ref[...]
+
+    @pl.when(away)
+    def _():
+        ids_copy(0, swap).start()
+        ids_copy(1, partner).start()
+
     target_load = pltpu.make_async_copy(target_ref, target, local_sem.at[2])
 
     packed[0, :, pl.ds(owner_at, owner_span), :] = model_ref[...].astype(BF)
@@ -413,7 +443,6 @@
 
     pack_copy().start()
     own_load.start()
-    emb_load.start()
     pl.when(home)(target_load.start)
     pack_copy().wait_recv()
 
@@ -435,36 +464,75 @@
         g_along(d, z).start()
     g_beside(0, z).start()
     g_partner(0, z).start()
-    pl.when(home)(emb_copy().start)
     for group in range(2):
         pl.when(away)(cross_copy(group).wait_recv)
         for d in range(1, n_z):
             model_along(group, d, z).start()
         model_beside(group, 0, z).start()
         model_partner(group, 0, z).start()
-
-    @pl.when(away)
-    def _():
-        emb_copy().start()
-        target_copy().start()
-
-    for d in range(1, n_z):
+    pl.when(away)(target_copy().start)
+
+    ids_copy(1, across).wait_recv()
+    pl.when(away)(ids_copy(0, swap).wait_recv)
+    ids_load = pltpu.make_async_copy(ids_in, ids, local_sem.at[3])
+    ids_load.start()
+    ids_load.wait()
+    table_load.wait()
+    sublane = lax.broadcasted_iota(jnp.int32, (8, half), 0)
+
+    def pick(slot, first, count, target_rows):
+        def block(i, carry):
+            at = (first + i) * 16
+            eights = []
+            for group in range(2):
+                value = jnp.zeros((8, half), F32)
+                for r in range(8):
+                    token = ids[slot, 0, at + group * 8 + r]
+                    aligned = token // 8
+                    tile = table[aligned].astype(F32)
+                    found = jnp.where(sublane == token - 8 * aligned, tile, 0.0)
+                    line = jnp.sum(found, axis=0, keepdims=True)
+                    value = jnp.where(sublane == r, line, value)
+                eights.append(value)
+            target_rows(
+                pl.ds(pl.multiple_of(at, 16), 16), jnp.concatenate(eights, axis=0).astype(BF)
+            )
+            return carry
+
+        lax.fori_loop(0, count, block, 0)
+
+    def to_across(at, value):
+        emb_out[at, :] = value
+
+    def to_own(at, value):
+        emb[at, emb_columns] = value
+
+    n_blocks = rows // 16
+    piece = n_blocks // 4
+
+    def g_relay(d):
         row = behind(d)
         g_along(d, row).wait_recv()
         g_beside(0, row).start()
         g_partner(0, row).start()
+
+    pick(1, 0, piece, to_across)
+    pick(1, piece, piece, to_across)
+    g_relay(1)
+    pick(1, 2 * piece, piece, to_across)
+    for d in range(2, n_z):
+        g_relay(d)
+    pick(1, 3 * piece, n_blocks - 3 * piece, to_across)
+    emb_copy().start()
     for row in range(n_z):
+        pick(0, row * piece, piece if row < 3 else n_blocks - 3 * piece, to_own)
         g_beside(1, row).wait_recv()
         g_partner(1, row).start()
-    for line in range(2):
-        for row in range(n_z):
-            g_partner(line, row).wait_recv()
-    for d in range(1, n_z):
-        g_along(d, z).wait_send()
-    for row in range(n_z):
-        g_beside(0, row).wait_send()
-        for line in range(2):
-            g_partner(line, row).wait_send()
+    g_arrived = g_rows.at[:, pl.ds(pl.multiple_of(jnp.where(home, quarter, 0), quarter), quarter), :]
+    remote(g_arrived, g_arrived, "gp", 0, partner).wait_recv()
+    all_sent(g_rows.at[:, g_own, pl.ds(0, (n_z - 1) * span)], "gz")
+    all_sent(g_rows.at[:, g_own, pl.ds(0, n_z * span)], "gy")
+    all_sent(g_rows.at[:, g_own, :], "gp")
     own_load.wait()
 
     chunk = half // 6
@@ -487,7 +555,6 @@
         def _():
             corr_copy(part).start()
 
-    emb_load.wait()
     emb_copy().wait_recv()
     block = rows // 5
 
@@ -515,9 +582,9 @@
             model_partner(group, 1, row).start()
 
     def arrive(group):
-        for line in range(2):
-            for row in range(n_z):
-                model_partner(group, line, row).wait_recv()
+        first, count = groups[group]
+        window = model.at[pl.ds(first, count), other_rows, :]
+        remote(window, window, "mp", group, partner).wait_recv()
 
     relay(0)
     settle(0)
@@ -649,23 +716,23 @@
     local_step(0, model, update, lambda k: None)
     pack_copy().wait_send()
     emb_copy().wait_send()
-    for group in range(2):
-        pl.when(home)(cross_copy(group).wait_send)
-        for d in range(1, n_z):
-            model_along(group, d, z).wait_send()
-        for row in range(n_z):
-            model_beside(group, 0, row).wait_send()
-            for line in range(2):
-                model_partner(group, line, row).wait_send()
+    ids_copy(1, across).wait_send()
+    all_sent(model.at[:, own_rows, pl.ds(0, (n_z - 1) * span)], "mz")
+    all_sent(model.at[:, own_rows, pl.ds(0, n_z * span)], "my")
+    all_sent(model.at[:, own_rows, :], "mp")
+
+    @pl.when(home)
+    def _():
+        all_sent(model.at[:, own_rows, columns(p)], "cross")
 
     @pl.when(away)
     def _():
+        ids_copy(0, swap).wait_send()
         target_copy().wait_send()
-        for part in range(parts):
-            corr_copy(part).wait_send()
-
-    for part in range(parts):
-        current_copy(part).wait_recv()
+        all_sent(corr, "corr")
+
+    arrived = current.at[:, other_rows, :]
+    remote(arrived, arrived, "cur", 0, partner).wait_recv()
     weight = weights_ref[client].astype(F32)
     taken = steps_ref[client].astype(F32)
     inverse = 1.0 / taken
@@ -727,18 +794,12 @@
 
     def gather_z(k):
         part, s = place(k)
+        arrived = z_in.at[k, pl.ds(1, n_z - 1)]
+        remote(arrived, arrived, "rz", k, partner).wait_recv()
         value = kept[k, z].astype(F32)
         for d in range(1, n_z):
-            z_copy(k, d).wait_recv()
             value += z_in[k, d].astype(F32)
         summed[part, sub_rows(s), :] = value
-        y_copy(k).wait_send()
-        for d in range(1, n_z):
-            z_copy(k, d).wait_send()
-        share_copy(part, s).wait_send()
-        grad_store(part, s).wait()
-        pl.when(away)(return_copy(part, s).wait_send)
-
         @pl.when(s == n_sub - 1)
         def _():
             final[part] = summed[part].T
@@ -764,8 +825,7 @@
             gather_z(k - z_lag)
 
     local_step(1, current, collect, advance)
-    for part in range(parts):
-        current_copy(part).wait_send()
+    all_sent(current.at[:, own_rows, :], "cur")
 
     def loop(k, carry):
         advance(k)
@@ -782,24 +842,42 @@
     step_total = step_total.astype(F32)
     control = control_ref[...]
     lost = step_total * (control - control.astype(BF).astype(F32))
-    for part in range(parts):
-        final_copy(part).wait_recv()
+    remote(final_in, final_in, "final", 0, partner).wait_recv()
     mine = final[:, pl.ds(owner_at, owner_span), :]
     theirs = final_in[...]
     step_out[...] = (jnp.where(b == 0, mine, theirs) + lost) / weight_total
     control_out[...] = jnp.where(b == 0, theirs, mine) / weight_total
 
-    for part in range(parts):
-        final_copy(part).wait_send()
-
-
-def widen_kernel(step_ref, control_ref, grad_ref, step_out, control_out, grad_out):
-    @pl.when(pl.program_id(0) == 0)
+    all_sent(final_in, "final")
+    all_sent(y_out, "ry")
+    all_sent(z_in.at[:, pl.ds(1, n_z - 1)], "rz")
+    all_sent(term_out, "share")
+
+    @pl.when(away)
     def _():
-        step_out[...] = step_ref[...]
-        control_out[...] = control_ref[...]
-
-    grad_out[...] = grad_ref[...].astype(F32)
+        all_sent(role_corr, "ret")
+
+    pltpu.make_async_copy(term_in, grad_out, local_sem.at[4]).wait()
+
+
+def widen_kernel(step_ref, control_ref, grad_ref, step_out, control_out, grad_out, narrow, wide, sem):
+    pieces = grad_ref.shape[0]
+    loads = [
+        pltpu.make_async_copy(grad_ref.at[i], narrow.at[i], sem.at[0, i]) for i in range(pieces)
+    ]
+    stores = [
+        pltpu.make_async_copy(wide.at[i], grad_out.at[i], sem.at[1, i]) for i in range(pieces)
+    ]
+    for load in loads:
+        load.start()
+    step_out[...] = step_ref[...]
+    control_out[...] = control_ref[...]
+    for i in range(pieces):
+        loads[i].wait()
+        wide[i] = narrow[i].astype(F32)
+        stores[i].start()
+    for store in stores:
+        store.wait()
 
 
 def paired_body(
@@ -823,20 +901,13 @@
     depth = 2 * half
     sub = 64
     n_chunks = parts * (half // sub)
-    pairs = [(c, f) for c in range(n_clients) for f in range(2)]
-    to_role = [(c * 2 + f, (c - c % 2 + f) * 2 + c % 2) for c, f in pairs]
-    to_across = [(c * 2 + f, (c - c % 2 + f) * 2 + 1 - c % 2) for c, f in pairs]
-    ids = jnp.concatenate(
-        [
-            lax.ppermute(token_ids[0], ("clients", "fsdp"), to_role),
-            lax.ppermute(token_ids[0], ("clients", "fsdp"), to_across),
-        ]
-    )
-    emb_columns = embedding.at[ids].get(mode="promise_in_bounds")
-
-    n_sem = 5 + 6 * n_z + 3 * n_pos + 5 * parts + n_chunks * (3 + n_z)
+    arrivals, n_send = semaphore_counts(parts, n_z, n_chunks)
     vmem = pltpu.VMEM
     scratch = [
+        vmem((embedding.shape[0] // 8, 8, half), BF),
+        vmem((2, 1, rows), jnp.int32),
+        pltpu.SMEM((2, 1, rows), jnp.int32),
+        vmem((rows, half), BF),
         vmem((2, parts, span, half), BF),
         vmem((parts, depth, width), BF),
         vmem((parts, depth, width), BF),
@@ -865,9 +936,9 @@
         vmem((parts, half, span), F32),
         vmem((parts, span, half), F32),
         vmem((parts, owner_span, half), F32),
-        pltpu.SemaphoreType.DMA((3 + n_chunks,)),
-        pltpu.SemaphoreType.DMA((n_sem,)),
-        pltpu.SemaphoreType.DMA((n_sem,)),
+        pltpu.SemaphoreType.DMA((5,)),
+        pltpu.SemaphoreType.DMA((n_send,)),
+        pltpu.SemaphoreType.DMA((sum(arrivals.values()),)),
     ]
     smem = pl.BlockSpec(memory_space=pltpu.SMEM)
     anywhere = pl.BlockSpec(memory_space=pl.ANY)
@@ -879,7 +950,7 @@
             jax.ShapeDtypeStruct((parts, owner_span, half), F32),
             jax.ShapeDtypeStruct((parts, half, width), BF),
         ),
-        in_specs=[smem, smem, anywhere, anywhere, inside, inside, inside, anywhere],
+        in_specs=[smem, smem, inside, anywhere, anywhere, inside, inside, inside, anywhere],
         out_specs=(inside, inside, anywhere),
         scratch_shapes=scratch,
         compiler_params=pltpu.CompilerParams(
@@ -888,27 +959,31 @@
     )(
         local_steps,
         client_weight,
-        emb_columns,
+        token_ids,
+        embedding.reshape(-1, 8, half),
         target[0],
         norm_gain,
         jnp.swapaxes(global_model, 1, 2),
         jnp.swapaxes(global_control, 1, 2),
         client_control[0],
     )
-    block = half // 2
-    small = pl.BlockSpec((parts, owner_span, half), lambda i: (0, 0, 0))
-    large = pl.BlockSpec((block, width), lambda i: (i, 0))
+    pieces = 2 * parts
+    block = parts * half // pieces
     step_sum, control_sum, update = pl.pallas_call(
         widen_kernel,
         out_shape=(
             jax.ShapeDtypeStruct((parts, owner_span, half), F32),
             jax.ShapeDtypeStruct((parts, owner_span, half), F32),
-            jax.ShapeDtypeStruct((parts * half, width), F32),
+            jax.ShapeDtypeStruct((pieces, block, width), F32),
         ),
-        grid=(parts * half // block,),
-        in_specs=[small, small, large],
-        out_specs=(small, small, large),
-    )(step_sum, control_sum, grad_rows.reshape(parts * half, width))
+        in_specs=[inside, inside, anywhere],
+        out_specs=(inside, inside, anywhere),
+        scratch_shapes=[
+            vmem((pieces, block, width), BF),
+            vmem((pieces, block, width), F32),
+            pltpu.SemaphoreType.DMA((2, pieces)),
+        ],
+    )(step_sum, control_sum, grad_rows.reshape(pieces, block, width))
     return (
         jnp.swapaxes(step_sum, 1, 2),
         jnp.swapaxes(control_sum, 1, 2),

time: 148 us -> 135 us (0.912)
  local copies, waits for them, and re-layouts: 10.6 us -> 0 us
  starting transfers between devices: 4.9 us -> 0 us
  Pallas kernels: 130 us -> 134 us
    gather x1 -> x0, local copies, waits for them, and re-layouts: 10.6 us -> none  [paired_body(): emb_columns = embedding.at[ids].get(mode='promise_in_bounds')]
    pallas_call x1, Pallas kernels: 124 us -> 129 us  [paired_body(): pl.pallas_call(functools.partial(round_kernel, n_z), out_shape=(jax.Shape...]
    ppermute x2 -> x0, starting transfers between devices: 4.9 us -> none  [the longest x1 4.24 us: paired_body(): lax.ppermute(token_ids[0], ('clients', 'fsdp'), to_across)]
  transfers between devices with their start and end apart: 2 -> 0, of which waited for: 1 -> 0; matrix products, arithmetic and copies ran while one was open for 0% -> 0% of each run, Pallas kernels for 0% -> 0%
where the time goes in v4:
time: 135 us
  Pallas kernels  134 us (99%)
    pallas_call x1, Pallas kernels, paired_body(): pl.pallas_call(functools.partial(round_kernel, n_z), out_shape=(jax.Shape...  129 us
    pallas_call x1, Pallas kernels, paired_body(): pl.pallas_call(widen_kernel, out_shape=(jax.ShapeDtypeStruct((parts, owne...  5.19 us

profile of v4, /device:TPU:0, one launch (start us, length us, event | category | flops | bytes accessed | tf_op | source)
XLA Modules:
  0.0 135.0 jit_solution(14155640278248198456)
XLA Ops:
  0.6 129.0 %shard_map.112 = (f32[3,64,384]{2,1,0:T(8,128)}, f32[3,64,384]{2,1,0:T(8,128)}, bf16[3,384,1024]{2,1,0:T(8,128)(2,1)}) custom-call(s32[16]{0:T(128)} %steps_ref.1, s32[16]{0:T(128)} %weights_ref.1, s32[1,640]{1,0:T(1,128)} %ids_ref.1, bf16[2048,8,384]{2,1,0:T(8,128)(2,1)} %bitcast.9, bf16[640,768]{1,0:T(8,128)(2,1)} %bitcast.12, f32[768]{0:T(1024)} %gain_ref.1, ...), custom_call_target="tpu_custom_call" | custom-call | tf_op jit(solution)/shard_map/pallas_call | solution.py:946
  129.6 5.2 %shard_map.113 = (f32[3,64,384]{2,1,0:T(8,128)}, f32[3,64,384]{2,1,0:T(8,128)}, f32[6,192,1024]{2,1,0:T(8,128)}) custom-call(f32[3,64,384]{2,1,0:T(8,128)} %get-tuple-element.9.step_ref, f32[3,64,384]{2,1,0:T(8,128)} %get-tuple-element.10.control_ref, bf16[6,192,1024]{2,1,0:T(8,128)(2,1)} %bitcast.11), custom_call_target="tpu_custom_call" | custom-call | tf_op jit(solution)/shard_map/pallas_call | solution.py:972

commit v5 on v4

--- a/solution.py
+++ b/solution.py
@@ -466,8 +466,6 @@
     g_partner(0, z).start()
     for group in range(2):
         pl.when(away)(cross_copy(group).wait_recv)
-        for d in range(1, n_z):
-            model_along(group, d, z).start()
         model_beside(group, 0, z).start()
         model_partner(group, 0, z).start()
     pl.when(away)(target_copy().start)
@@ -516,16 +514,27 @@
         g_beside(0, row).start()
         g_partner(0, row).start()
 
-    pick(1, 0, piece, to_across)
-    pick(1, piece, piece, to_across)
+    def relay(group, d):
+        row = behind(d)
+        model_along(group, d, row).wait_recv()
+        model_beside(group, 0, row).start()
+        model_partner(group, 0, row).start()
+
+    def launch(group):
+        for d in range(1, n_z):
+            model_along(group, d, z).start()
+
+    pick(1, 0, 2 * piece, to_across)
     g_relay(1)
-    pick(1, 2 * piece, piece, to_across)
+    launch(0)
+    pick(1, 2 * piece, n_blocks - 2 * piece, to_across)
+    emb_copy().start()
     for d in range(2, n_z):
         g_relay(d)
-    pick(1, 3 * piece, n_blocks - 3 * piece, to_across)
-    emb_copy().start()
+    launch(1)
     for row in range(n_z):
-        pick(0, row * piece, piece if row < 3 else n_blocks - 3 * piece, to_own)
+        if row < 2:
+            pick(0, row * piece, piece, to_own)
         g_beside(1, row).wait_recv()
         g_partner(1, row).start()
     g_arrived = g_rows.at[:, pl.ds(pl.multiple_of(jnp.where(home, quarter, 0), quarter), quarter), :]
@@ -555,6 +564,9 @@
         def _():
             corr_copy(part).start()
 
+    for d in range(1, n_z):
+        relay(0, d)
+    pick(0, 2 * piece, n_blocks - 2 * piece, to_own)
     emb_copy().wait_recv()
     block = rows // 5
 
@@ -569,13 +581,6 @@
 
     lax.fori_loop(0, 5, normalise, 0)
 
-    def relay(group):
-        for d in range(1, n_z):
-            row = behind(d)
-            model_along(group, d, row).wait_recv()
-            model_beside(group, 0, row).start()
-            model_partner(group, 0, row).start()
-
     def settle(group):
         for row in range(n_z):
             model_beside(group, 1, row).wait_recv()
@@ -586,9 +591,9 @@
         window = model.at[pl.ds(first, count), other_rows, :]
         remote(window, window, "mp", group, partner).wait_recv()
 
-    relay(0)
     settle(0)
-    relay(1)
+    for d in range(1, n_z):
+        relay(1, d)
     arrive(0)
 
     loss_scale = 1.0 / math.sqrt(2 * rows)
@@ -860,22 +865,23 @@
     pltpu.make_async_copy(term_in, grad_out, local_sem.at[4]).wait()
 
 
-def widen_kernel(step_ref, control_ref, grad_ref, step_out, control_out, grad_out, narrow, wide, sem):
+def widen_kernel(
+    step_ref, control_ref, grad_ref, step_out, control_out, grad_out, narrow, wide, small, sem
+):
     pieces = grad_ref.shape[0]
-    loads = [
-        pltpu.make_async_copy(grad_ref.at[i], narrow.at[i], sem.at[0, i]) for i in range(pieces)
-    ]
-    stores = [
-        pltpu.make_async_copy(wide.at[i], grad_out.at[i], sem.at[1, i]) for i in range(pieces)
-    ]
+    pairs = [(step_ref, small.at[0]), (control_ref, small.at[1])]
+    pairs += [(grad_ref.at[i], narrow.at[i]) for i in range(pieces)]
+    loads = [pltpu.make_async_copy(src, dst, sem.at[0, i]) for i, (src, dst) in enumerate(pairs)]
+    pairs = [(small.at[0], step_out), (small.at[1], control_out)]
+    pairs += [(wide.at[i], grad_out.at[i]) for i in range(pieces)]
+    stores = [pltpu.make_async_copy(src, dst, sem.at[1, i]) for i, (src, dst) in enumerate(pairs)]
     for load in loads:
         load.start()
-    step_out[...] = step_ref[...]
-    control_out[...] = control_ref[...]
-    for i in range(pieces):
-        loads[i].wait()
-        wide[i] = narrow[i].astype(F32)
-        stores[i].start()
+    for i, (load, store) in enumerate(zip(loads, stores)):
+        load.wait()
+        if i >= 2:
+            wide[i - 2] = narrow[i - 2].astype(F32)
+        store.start()
     for store in stores:
         store.wait()
 
@@ -976,12 +982,13 @@
             jax.ShapeDtypeStruct((parts, owner_span, half), F32),
             jax.ShapeDtypeStruct((pieces, block, width), F32),
         ),
-        in_specs=[inside, inside, anywhere],
-        out_specs=(inside, inside, anywhere),
+        in_specs=[anywhere, anywhere, anywhere],
+        out_specs=(anywhere, anywhere, anywhere),
         scratch_shapes=[
             vmem((pieces, block, width), BF),
             vmem((pieces, block, width), F32),
-            pltpu.SemaphoreType.DMA((2, pieces)),
+            vmem((2, parts, owner_span, half), F32),
+            pltpu.SemaphoreType.DMA((2, pieces + 2)),
         ],
     )(step_sum, control_sum, grad_rows.reshape(pieces, block, width))
     return (

time: 135 us -> 129 us (0.956)
  Pallas kernels: 134 us -> 128 us
    pallas_call x1, Pallas kernels: 129 us -> 124 us  [paired_body(): pl.pallas_call(functools.partial(round_kernel, n_z), out_shape=(jax.Shape...]
    pallas_call x1, Pallas kernels: 5.19 us -> 3.54 us  [paired_body(): pl.pallas_call(widen_kernel, out_shape=(jax.ShapeDtypeStruct((parts, owne...]
where the time goes in v5:
time: 129 us
  Pallas kernels  128 us (99%)
    pallas_call x1, Pallas kernels, paired_body(): pl.pallas_call(functools.partial(round_kernel, n_z), out_shape=(jax.Shape...  124 us
    pallas_call x1, Pallas kernels, paired_body(): pl.pallas_call(widen_kernel, out_shape=(jax.ShapeDtypeStruct((parts, owne...  3.54 us

profile of v5, /device:TPU:0, one launch (start us, length us, event | category | flops | bytes accessed | tf_op | source)
XLA Modules:
  0.0 128.5 jit_solution(16814631437855897795)
XLA Ops:
  0.6 124.2 %shard_map.112 = (f32[3,64,384]{2,1,0:T(8,128)}, f32[3,64,384]{2,1,0:T(8,128)}, bf16[3,384,1024]{2,1,0:T(8,128)(2,1)}) custom-call(s32[16]{0:T(128)} %steps_ref.1, s32[16]{0:T(128)} %weights_ref.1, s32[1,640]{1,0:T(1,128)} %ids_ref.1, bf16[2048,8,384]{2,1,0:T(8,128)(2,1)} %bitcast.9, bf16[640,768]{1,0:T(8,128)(2,1)} %bitcast.12, f32[768]{0:T(1024)} %gain_ref.1, ...), custom_call_target="tpu_custom_call" | custom-call | tf_op jit(solution)/shard_map/pallas_call | solution.py:952
  124.8 3.5 %shard_map.113 = (f32[3,64,384]{2,1,0:T(8,128)}, f32[3,64,384]{2,1,0:T(8,128)}, f32[6,192,1024]{2,1,0:T(8,128)}) custom-call(f32[3,64,384]{2,1,0:T(8,128)} %get-tuple-element.9.step_ref, f32[3,64,384]{2,1,0:T(8,128)} %get-tuple-element.10.control_ref, bf16[6,192,1024]{2,1,0:T(8,128)(2,1)} %bitcast.11), custom_call_target="tpu_custom_call" | custom-call | tf_op jit(solution)/shard_map/pallas_call | solution.py:978

commit v6 on v5

--- a/solution.py
+++ b/solution.py
@@ -284,6 +284,38 @@
     def behind(d):
         return lax.rem(z + n_z - d, n_z)
 
+    hop = n_z == 4
+
+    def turn(i):
+        return jnp.where(z == 0, n_z - i, i) if hop else i
+
+    def send_tiles(copy):
+        for d in range(1, n_z):
+            if not hop or d == 2:
+                copy(d, z).start()
+            else:
+                pl.when(z != (n_z - 1 if d == 1 else 0))(copy(d, z).start)
+
+    def hop_tile(copy, d, row):
+        if hop:
+            pl.when((d == 2) & (z == 1))(copy(1, row, -1).start)
+            pl.when((d == 2) & (z == 2))(copy(3, row, 1).start)
+
+    def along_sent(window, name):
+        if hop:
+            ends = (z == 0) | (z == n_z - 1)
+
+            @pl.when(ends)
+            def _():
+                all_sent(window(n_z - 2), name)
+
+            @pl.when(jnp.logical_not(ends))
+            def _():
+                all_sent(window(n_z), name)
+
+        else:
+            all_sent(window(n_z - 1), name)
+
     def position(line, row):
         return 2 * row + (y if line == 0 else 1 - y)
 
@@ -341,9 +373,9 @@
         first, count = groups[group]
         return model.at[pl.ds(first, count), own_rows, columns(pos)]
 
-    def g_along(d, row):
+    def g_along(d, row, step=None):
         window = g_window(position(0, row))
-        return remote(window, window, "gz", d, along(d))
+        return remote(window, window, "gz", d, along(d) if step is None else along(step + n_z))
 
     def g_beside(line, row):
         window = g_window(position(line, row))
@@ -357,9 +389,12 @@
         window = model_window(group, p)
         return remote(window, window, "cross", group, across)
 
-    def model_along(group, d, row):
+    def model_along(group, d, row, step=None):
         window = model_window(group, position(0, row))
-        return remote(window, window, "mz", group * n_z + d, along(d))
+        return remote(
+            window, window, "mz", group * n_z + d,
+            along(d) if step is None else along(step + n_z),
+        )
 
     def model_beside(group, line, row):
         window = model_window(group, position(line, row))
@@ -460,8 +495,7 @@
         for part in range(parts):
             g_rows[part, quarter:, columns(p)] = packed[1, part].T[quarter:]
 
-    for d in range(1, n_z):
-        g_along(d, z).start()
+    send_tiles(g_along)
     g_beside(0, z).start()
     g_partner(0, z).start()
     for group in range(2):
@@ -508,21 +542,24 @@
     n_blocks = rows // 16
     piece = n_blocks // 4
 
-    def g_relay(d):
+    def g_relay(i):
+        d = turn(i)
         row = behind(d)
         g_along(d, row).wait_recv()
+        hop_tile(g_along, d, row)
         g_beside(0, row).start()
         g_partner(0, row).start()
 
-    def relay(group, d):
+    def relay(group, i):
+        d = turn(i)
         row = behind(d)
         model_along(group, d, row).wait_recv()
+        hop_tile(functools.partial(model_along, group), d, row)
         model_beside(group, 0, row).start()
         model_partner(group, 0, row).start()
 
     def launch(group):
-        for d in range(1, n_z):
-            model_along(group, d, z).start()
+        send_tiles(functools.partial(model_along, group))
 
     pick(1, 0, 2 * piece, to_across)
     g_relay(1)
@@ -539,7 +576,7 @@
         g_partner(1, row).start()
     g_arrived = g_rows.at[:, pl.ds(pl.multiple_of(jnp.where(home, quarter, 0), quarter), quarter), :]
     remote(g_arrived, g_arrived, "gp", 0, partner).wait_recv()
-    all_sent(g_rows.at[:, g_own, pl.ds(0, (n_z - 1) * span)], "gz")
+    along_sent(lambda count: g_rows.at[:, g_own, pl.ds(0, count * span)], "gz")
     all_sent(g_rows.at[:, g_own, pl.ds(0, n_z * span)], "gy")
     all_sent(g_rows.at[:, g_own, :], "gp")
     own_load.wait()
@@ -722,7 +759,7 @@
     pack_copy().wait_send()
     emb_copy().wait_send()
     ids_copy(1, across).wait_send()
-    all_sent(model.at[:, own_rows, pl.ds(0, (n_z - 1) * span)], "mz")
+    along_sent(lambda count: model.at[:, own_rows, pl.ds(0, count * span)], "mz")
     all_sent(model.at[:, own_rows, pl.ds(0, n_z * span)], "my")
     all_sent(model.at[:, own_rows, :], "mp")
 

time: 129 us -> 122 us (0.946)
  Pallas kernels: 128 us -> 121 us
    pallas_call x1, Pallas kernels: 124 us -> 117 us  [paired_body(): pl.pallas_call(functools.partial(round_kernel, n_z), out_shape=(jax.Shape...]
where the time goes in v6:
time: 122 us; the launch traced here: 121 us
  Pallas kernels  121 us (99%)
    pallas_call x1, Pallas kernels, paired_body(): pl.pallas_call(functools.partial(round_kernel, n_z), out_shape=(jax.Shape...  117 us
    pallas_call x1, Pallas kernels, paired_body(): pl.pallas_call(widen_kernel, out_shape=(jax.ShapeDtypeStruct((parts, owne...  3.54 us

profile of v6, /device:TPU:0, one launch (start us, length us, event | category | flops | bytes accessed | tf_op | source)
XLA Modules:
  0.0 121.5 jit_solution(9396752719091400068)
XLA Ops:
  0.6 117.1 %shard_map.112 = (f32[3,64,384]{2,1,0:T(8,128)}, f32[3,64,384]{2,1,0:T(8,128)}, bf16[3,384,1024]{2,1,0:T(8,128)(2,1)}) custom-call(s32[16]{0:T(128)} %steps_ref.1, s32[16]{0:T(128)} %weights_ref.1, s32[1,640]{1,0:T(1,128)} %ids_ref.1, bf16[2048,8,384]{2,1,0:T(8,128)(2,1)} %bitcast.9, bf16[640,768]{1,0:T(8,128)(2,1)} %bitcast.12, f32[768]{0:T(1024)} %gain_ref.1, ...), custom_call_target="tpu_custom_call" | custom-call | tf_op jit(solution)/shard_map/pallas_call | solution.py:989
  117.8 3.5 %shard_map.113 = (f32[3,64,384]{2,1,0:T(8,128)}, f32[3,64,384]{2,1,0:T(8,128)}, f32[6,192,1024]{2,1,0:T(8,128)}) custom-call(f32[3,64,384]{2,1,0:T(8,128)} %get-tuple-element.9.step_ref, f32[3,64,384]{2,1,0:T(8,128)} %get-tuple-element.10.control_ref, bf16[6,192,1024]{2,1,0:T(8,128)(2,1)} %bitcast.11), custom_call_target="tpu_custom_call" | custom-call | tf_op jit(solution)/shard_map/pallas_call | solution.py:1015

commit v7 on v6

--- a/solution.py
+++ b/solution.py
@@ -847,7 +847,7 @@
             final[part] = summed[part].T
             final_copy(part).start()
 
-    split_lag, y_lag, z_lag = 1, 3, 6
+    split_lag, y_lag, z_lag = 1, 4, 8
 
     def advance(k):
         @pl.when(k < n_chunks)

time: 122 us -> 122 us (level)
  no operation moved by 1% of the time
where the time goes in v7:
time: 122 us; the launch traced here: 121 us
  Pallas kernels  121 us (99%)
    pallas_call x1, Pallas kernels, paired_body(): pl.pallas_call(functools.partial(round_kernel, n_z), out_shape=(jax.Shape...  117 us
    pallas_call x1, Pallas kernels, paired_body(): pl.pallas_call(widen_kernel, out_shape=(jax.ShapeDtypeStruct((parts, owne...  3.54 us

profile of v7, /device:TPU:0, one launch (start us, length us, event | category | flops | bytes accessed | tf_op | source)
XLA Modules:
  0.0 121.5 jit_solution(8983793918970885171)
XLA Ops:
  0.6 117.1 %shard_map.112 = (f32[3,64,384]{2,1,0:T(8,128)}, f32[3,64,384]{2,1,0:T(8,128)}, bf16[3,384,1024]{2,1,0:T(8,128)(2,1)}) custom-call(s32[16]{0:T(128)} %steps_ref.1, s32[16]{0:T(128)} %weights_ref.1, s32[1,640]{1,0:T(1,128)} %ids_ref.1, bf16[2048,8,384]{2,1,0:T(8,128)(2,1)} %bitcast.9, bf16[640,768]{1,0:T(8,128)(2,1)} %bitcast.12, f32[768]{0:T(1024)} %gain_ref.1, ...), custom_call_target="tpu_custom_call" | custom-call | tf_op jit(solution)/shard_map/pallas_call | solution.py:989
  117.8 3.5 %shard_map.113 = (f32[3,64,384]{2,1,0:T(8,128)}, f32[3,64,384]{2,1,0:T(8,128)}, f32[6,192,1024]{2,1,0:T(8,128)}) custom-call(f32[3,64,384]{2,1,0:T(8,128)} %get-tuple-element.9.step_ref, f32[3,64,384]{2,1,0:T(8,128)} %get-tuple-element.10.control_ref, bf16[6,192,1024]{2,1,0:T(8,128)(2,1)} %bitcast.11), custom_call_target="tpu_custom_call" | custom-call | tf_op jit(solution)/shard_map/pallas_call | solution.py:1015
